TPU v7x, 256 devices: a whole 4x4x8 slice. The times are simulated.
256 devices in a mesh: row: 8 (over y, core), col: 32 (over z, x).
Axes of the slice: x: 4, y: 4, z: 8, core: 2. Of those that a mesh axis runs over, the one named last changes fastest.
Arguments:
- fock: float32 [2, 8192, 8192], P(None, 'row', 'col'), may hold values from -1.1875 to 1.1875, as said below
- density: float32 [2, 8192, 8192], P(None, 'row', 'col'), may hold values from -1.09375 to 1.09375, as said below
- probe: float32 [2, 8192, 128], P(None, 'col'), may hold values from -6 to 6
Outputs:
- propagated: float32 [2, 8192, 128], P(None, 'col')
Inputs may be any that keep to these rules, and one draw needn't show every extreme that they name: Hermitian: fock[0] is symmetric and fock[1] antisymmetric, exactly. Hermitian: density[0] is symmetric and density[1] antisymmetric, exactly.
All inputs are finite; a program needn't handle non-finite values.
Results may differ from a plain program's by a relative error of at most 0.00011.
Values sent between devices are 32-bit elements; how exact they have to be, the bound alone decides.
A program may use at most 64 MiB of HBM per device.

v0:
```python
import jax
import jax.numpy as jnp
from jax import lax
from jax.sharding import PartitionSpec as P

time_step = 0.5


def split_up(x, dim, peers):
    before, after = (x.shape[:dim], x.shape[dim + 1 :])
    return jnp.moveaxis(x.reshape(*before, peers, -1, *after), dim, 0)


def sum_at_owner(x, axis, dim):
    pieces = split_up(x, dim, lax.axis_size(axis))
    arrived = lax.all_to_all(pieces, axis, split_axis=0, concat_axis=0, tiled=True)
    return arrived.sum(axis=0)


def from_everyone(x, axis):
    copies = jnp.broadcast_to(x, (lax.axis_size(axis), *x.shape))
    return lax.all_to_all(copies, axis, split_axis=0, concat_axis=0, tiled=True)


def joined_along(pieces, dim):
    pieces = jnp.moveaxis(pieces, 0, dim)
    shape = pieces.shape
    return pieces.reshape(*shape[:dim], shape[dim] * shape[dim + 1], *shape[dim + 2 :])


def gather_directly(x, axis, dim):
    pieces = from_everyone(x, axis)
    return joined_along(pieces, dim)


def picked(x, axis, root):
    return lax.dynamic_index_in_dim(lax.all_gather(x, axis), root, 0, keepdims=False)


def of_everyone(x, axis):
    everything = from_everyone(x, axis)
    return jnp.sum(everything, axis=0)


def plain_dot(left, right):
    return jnp.dot(left, right, precision=lax.Precision.HIGHEST, preferred_element_type=jnp.float32)


def adjoint_dot(left, right):
    return lax.dot_general(
        left,
        right,
        (((0,), (0,)), ((), ())),
        precision=lax.Precision.HIGHEST,
        preferred_element_type=jnp.float32,
    )


def prepare(matrix, adjoint):
    real_m = matrix[0]
    imag_m = -matrix[1] if adjoint else matrix[1]
    return (real_m, imag_m, real_m + imag_m, imag_m - real_m)


def complex_product(pieces, vector, adjoint):
    multiply = adjoint_dot if adjoint else plain_dot
    real_m, imag_m, sum_m, diff_m = pieces
    real_v = vector[0]
    imag_v = vector[1]
    first = multiply(real_m, real_v + imag_v)
    second = multiply(sum_m, imag_v)
    third = multiply(diff_m, real_v)
    return jnp.stack([first - second, first + third])


def times_imag(vector, factor):
    return jnp.stack([-factor * vector[1], factor * vector[0]])


def shards(fock, density, probe):
    rows_block = fock.shape[1]
    cols_block = fock.shape[2]
    fock_plain = prepare(fock, False)
    fock_adjoint = prepare(fock, True)
    density_plain = prepare(density, False)

    def reduce_cols(partial_value):
        share = sum_at_owner(partial_value, "col", 1)
        return gather_directly(share, "col", 1)

    def to_columns(vector):
        column = lax.axis_index("col")
        source = column * cols_block // rows_block
        offset = column * cols_block - source * rows_block
        piece = lax.dynamic_slice_in_dim(vector, offset, cols_block, 1)
        return picked(piece, "row", source)

    def forward(pieces, vector):
        return reduce_cols(complex_product(pieces, vector, False))

    def backward(pieces, vector):
        return of_everyone(complex_product(pieces, vector, True), "row")

    def alternate(vector, in_columns, sign):
        current = vector
        column_sum = vector if in_columns else None
        row_sum = None if in_columns else vector
        if in_columns:
            current = forward(fock_plain, current)
        else:
            current = backward(fock_adjoint, current)
        in_columns = not in_columns
        current = times_imag(current, sign * time_step / 1)
        if in_columns:
            column_sum = current
        else:
            row_sum = current
        return (column_sum, row_sum)

    column_sum, row_sum = alternate(probe, True, 1.0)
    first = column_sum + to_columns(row_sum)
    second = forward(density_plain, first)
    column_sum, row_sum = alternate(second, False, -1.0)
    result = column_sum + to_columns(row_sum)
    return result


def solution(mesh):
    return jax.shard_map(
        shards,
        mesh=mesh,
        in_specs=(P(None, "row", "col"), P(None, "row", "col"), P(None, "col", None)),
        out_specs=P(None, "col", None),
        check_vma=False,
    )
```

profile of v0, /device:TPU:1, one launch (start us, length us, event | category | flops | bytes accessed | tf_op | source)
XLA Modules:
  0.0 246.7 jit_solution(15786275144797775265)
XLA Ops:
  6.5 0.0 copy-start
  6.5 0.0 copy-start.2
  6.5 2.7 %convolution_bitcast_fusion.1 = f32[1024,128]{0,1:T(8,128)S(1)} fusion(f32[2,1024,256]{2,1,0:T(8,128)} %param.3, f32[2,256,128]{2,1,0:T(8,128)} %param.5), kind=kOutput, calls=%fused_computation.5 | convolution fusion | flops 402685952 | bytes 1835008 | tf_op jit(solution)/shard_map/dot_general | solution.py:46
  9.3 2.8 %convolution_subtract_fusion.1 = f32[1024,128]{0,1:T(8,128)S(1)} fusion(f32[1024,128]{0,1:T(8,128)S(1)} %convolution_bitcast_fusion.1, f32[2,1024,256]{2,1,0:T(8,128)} %param.3, f32[2,256,128]{2,1,0:T(8,128)} %param.5), kind=kOutput, calls=%fused_computation.3 | convolution fusion | flops 403046400 | bytes 3276800 | tf_op jit(solution)/shard_map/dot_general | solution.py:46
  12.1 0.0 copy-done
  12.1 0.0 copy-done.2
  12.1 1.3 convolution_add_fusion.1
  13.4 1.0 copy.50
  14.4 0.2 copy.52
  14.6 1.1 maximum_bitcast_fusion
  15.7 0.1 copy.53
  15.8 37.9 %all_to_all.25 = f32[32,2,32,128]{3,2,1,0:T(8,128)S(1)} all-to-all(f32[32,2,32,128]{3,2,1,0:T(8,128)S(1)} %copy.53), channel_id=1, replica_groups=mesh['row'=8,'col'=32] {'col'}, dimensions={0} | all-to-all | bytes 2097152 | tf_op jit(solution)/shard_map/all_to_all | solution.py:16
  53.6 0.1 reduce_sum.27
  53.7 1.1 broadcast_in_dim.9
  54.8 6.4 %all-to-all-start.1 = ((f32[32,2,32,128]{3,2,1,0:T(8,128)}), f32[32,2,32,128]{3,2,1,0:T(8,128)S(1)}, u32[]{:S(2)}, u32[]{:S(2)}) async-start(f32[32,2,32,128]{3,2,1,0:T(8,128)} %broadcast_in_dim.9), calls=%async_computation.1 | async-start | bytes 2097152 | tf_op jit(solution)/shard_map/all_to_all | solution.py:22
  61.2 0.0 all-gather.5.cloned.1.call-start
  61.3 25.3 %all-to-all-done.1 = f32[32,2,32,128]{3,2,1,0:T(8,128)S(1)} async-done(((f32[32,2,32,128]{3,2,1,0:T(8,128)}), f32[32,2,32,128]{3,2,1,0:T(8,128)S(1)}, u32[]{:S(2)}, u32[]{:S(2)}) %all-to-all-start.1) | async-done | bytes 1048608 | tf_op jit(solution)/shard_map/all_to_all | solution.py:22
  86.6 0.1 slice_multiply_fusion
  86.7 0.7 fusion.34
  87.4 0.0 all-gather.5.cloned.1.call-update
  87.5 0.0 all-gather.7.cloned.1.call-start
  87.5 28.5 %all-gather.5.cloned.1.call-done = f32[16,256,128]{2,1,0:T(8,128)} async-done(((f32[2,256,128]{2,1,0:T(8,128)}), f32[16,256,128]{2,1,0:T(8,128)}) %all-gather.5.cloned.1.call-update) | async-done | bytes 2097168 | tf_op jit(solution)/shard_map/all_gather | solution.py:37
  116.1 1.1 bitcast_add_fusion
  117.2 2.5 convolution_bitcast_fusion
  119.7 0.0 copy-done.1
  119.7 1.3 convolution_subtract_fusion
  121.0 1.3 convolution_add_fusion
  122.2 1.0 copy.55
  123.2 0.2 copy.57
  123.4 1.1 maximum_bitcast_fusion.1
  124.5 0.1 copy.58
  124.6 36.2 %all_to_all.26 = f32[32,2,32,128]{3,2,1,0:T(8,128)S(1)} all-to-all(f32[32,2,32,128]{3,2,1,0:T(8,128)S(1)} %copy.58), channel_id=1, replica_groups=mesh['row'=8,'col'=32] {'col'}, dimensions={0} | all-to-all | bytes 2097152 | tf_op jit(solution)/shard_map/all_to_all | solution.py:16
  160.8 0.1 reduce_sum.28
  160.9 0.1 broadcast_in_dim.10
  161.0 31.2 %all_to_all.27 = f32[32,2,32,128]{3,2,1,0:T(8,128)S(1)} all-to-all(f32[32,2,32,128]{3,2,1,0:T(8,128)S(1)} %broadcast_in_dim.10), channel_id=1, replica_groups=mesh['row'=8,'col'=32] {'col'}, dimensions={0} | all-to-all | bytes 2097152 | tf_op jit(solution)/shard_map/all_to_all | solution.py:22
  192.2 0.1 copy.71
  192.3 0.7 constant_dynamic-slice_fusion
  193.1 0.0 all-gather.7.cloned.1.call-update
  193.1 0.2 fusion.52
  193.3 1.0 convolution_bitcast_fusion.2
  194.3 1.1 fusion.1
  195.4 1.1 fusion
  196.5 0.1 copy.62
  196.6 0.2 broadcast_in_dim.11
  196.9 41.1 %all_to_all.28 = f32[8,2,256,128]{3,2,1,0:T(8,128)S(1)} all-to-all(f32[8,2,256,128]{3,2,1,0:T(8,128)S(1)} %broadcast_in_dim.11), channel_id=1, replica_groups=mesh['row'=8,'col'=32] {'row'}, dimensions={0} | all-to-all | bytes 4194304 | tf_op jit(solution)/shard_map/all_to_all | solution.py:22
  238.0 0.1 reduce_sum.29
  238.1 0.0 all-gather.7.cloned.1.call-done
  238.1 1.7 maximum_add_fusion
  (3 shorter events, 0.0 us)
Async XLA Ops:
  6.5 5.6 %copy-start = (f32[2,1024,256]{2,1,0:T(8,128)S(1)}, f32[2,1024,256]{2,1,0:T(8,128)}, u32[]{:S(2)}) copy-start(f32[2,1024,256]{2,1,0:T(8,128)} %param.3) | copy-start | bytes 6291460
  6.5 5.6 %copy-start.2 = (f32[2,256,128]{2,1,0:T(8,128)S(1)}, f32[2,256,128]{2,1,0:T(8,128)}, u32[]{:S(2)}) copy-start(f32[2,256,128]{2,1,0:T(8,128)} %param.5) | copy-start | bytes 786436
  54.8 31.8 %all-to-all-start.1 = ((f32[32,2,32,128]{3,2,1,0:T(8,128)}), f32[32,2,32,128]{3,2,1,0:T(8,128)S(1)}, u32[]{:S(2)}, u32[]{:S(2)}) async-start(f32[32,2,32,128]{3,2,1,0:T(8,128)} %broadcast_in_dim.9), calls=%async_computation.1 | async-start | bytes 2097152 | tf_op jit(solution)/shard_map/all_to_all | solution.py:22
  61.2 54.9 %all-gather.5.cloned.1.call-start = ((), (), s32[]{:S(2)}) async-start(), calls=%async_computation.5 | async-start | bytes 2359296 | tf_op jit(solution)/shard_map/all_gather | solution.py:37
  87.5 150.7 %all-gather.7.cloned.1.call-start = ((), (), s32[]{:S(2)}) async-start(), calls=%async_computation.6 | async-start | bytes 2359296 | tf_op jit(solution)/shard_map/all_gather | solution.py:37
  116.1 3.6 %copy-start.1 = (f32[2,1024,256]{2,1,0:T(8,128)S(1)}, f32[2,1024,256]{2,1,0:T(8,128)}, u32[]{:S(2)}) copy-start(f32[2,1024,256]{2,1,0:T(8,128)} %param.4) | copy-start | bytes 6291460
Sparse Core Ops, SparseCore 0:
  87.6 28.4 all-gather.4
  193.2 42.1 all-gather.6
where the time goes:
time: 247 us
  blocking collectives  146 us (59%)
  waiting for transfers between devices  53.9 us (22%)
  matrix products  15 us (6%)
  between operations  13.7 us (6%)
  starting transfers between devices  6.47 us (3%)
  other arithmetic  6.37 us (3%)
  local copies, waits for them, and re-layouts  4.88 us (2%)
    all_to_all x2, blocking collectives, sum_at_owner(): lax.all_to_all(pieces, axis, split_axis=0, concat_axis=0, tiled=True)  74 us
    all_to_all x2, blocking collectives, from_everyone(): return lax.all_to_all(copies, axis, split_axis=0, concat_axis=0, tiled=True)  72.3 us
    all_gather x2, waiting for transfers between devices, picked(): lax.all_gather(x, axis)  28.6 us
    all_to_all x1, waiting for transfers between devices, from_everyone(): return lax.all_to_all(copies, axis, split_axis=0, concat_axis=0, tiled=True)  25.3 us
    dot_general x6, matrix products, plain_dot(): jnp.dot(left, right, precision=lax.Precision.HIGHEST, preferred_element_t...  11.8 us
    all_to_all x1, starting transfers between devices, from_everyone(): return lax.all_to_all(copies, axis, split_axis=0, concat_axis=0, tiled=True)  6.38 us
  transfers between devices with their start and end apart: 3, of which 2 were waited for; matrix products, arithmetic and copies ran while one was open for 2% of the time, Pallas kernels for 0%

commit v1 on v0

v1 whole, which is shorter than its diff:
```python
import functools

import jax
import jax.numpy as jnp
from jax import lax
from jax.experimental import pallas as pl
from jax.experimental.pallas import tpu as pltpu
from jax.sharding import PartitionSpec as P

MESH = pl.DeviceIdType.MESH
DT = 0.5
GROUPS = 2
ROWS = 1024
COLS = 256
PIECES = 8
DEPTH = 16
WIDE = PIECES * DEPTH


def split(value):
    high = value.astype(jnp.bfloat16)
    return high, (value - high.astype(jnp.float32)).astype(jnp.bfloat16)


def prepare(matrix, high, low):
    def part(i, carry):
        rows = pl.ds(pl.multiple_of(i * COLS, COLS), COLS)
        for j in range(2):
            h, l = split(matrix[j, rows, :])
            high[rows, j * COLS : (j + 1) * COLS] = h
            low[rows, j * COLS : (j + 1) * COLS] = l
        return carry

    lax.fori_loop(0, ROWS // COLS, part, 0)


def factors(phase, vector):
    real, imag = vector[:, :8], vector[:, 8:]
    if phase == 1:
        first, second = (real, imag), (-imag, real)
    else:
        dt = DT if phase == 0 else -DT
        first, second = (-dt * imag, dt * real), (-dt * real, -dt * imag)
    first = jnp.concatenate(first, axis=1).reshape(WIDE, COLS)
    second = jnp.concatenate(second, axis=1).reshape(WIDE, COLS)
    return jnp.concatenate([first, second], axis=1)


def times(high, low, matrix_high, matrix_low):
    dot = functools.partial(
        lax.dot_general,
        dimension_numbers=(((1,), (1,)), ((), ())),
        preferred_element_type=jnp.float32,
    )
    return dot(high, matrix_high) + (dot(low, matrix_high) + dot(high, matrix_low))


def kernel(
    fock_hbm, density_hbm, probe_hbm, out,
    fock, density, probe, fock_high, fock_low, density_high, density_low,
    start, chunks, relay_a, relay_b, from_left, from_right, summed, arrived, gathered,
    load_sem, x_send, x_recv, z_send, z_recv, g_send, g_recv,
):
    row, col = lax.axis_index("row"), lax.axis_index("col")
    z, x = col // 4, lax.rem(col, 4)
    right = z * 4 + lax.rem(x + 1, 4)
    left = z * 4 + lax.rem(x + 3, 4)
    home = row * 4 + x
    at_home = row == z

    loads = [
        pltpu.make_async_copy(source, target, load_sem.at[i])
        for i, (source, target) in enumerate(
            ((probe_hbm, probe), (fock_hbm, fock), (density_hbm, density))
        )
    ]
    for load in loads:
        load.start()

    barrier = pltpu.get_barrier_semaphore()

    def hello(r, c):
        pl.semaphore_signal(barrier, inc=1, device_id=(r, c), device_id_type=MESH)

    hello(row, right)
    hello(row, left)
    for j in range(1, PIECES):
        hello(lax.rem(row + j, PIECES), col)
        hello(z, lax.rem(z + j, 8) * 4 + x)

    @pl.when(jnp.logical_not(at_home))
    def _():
        hello(z, col)

    loads[0].wait()
    for j in range(2):
        turned = probe[j].T
        for g in range(GROUPS):
            start[g, :, j * 8 : (j + 1) * 8, :] = turned[g * 64 : (g + 1) * 64].reshape(PIECES, 8, COLS)
    loads[1].wait()
    prepare(fock, fock_high, fock_low)

    sends = []

    def send(source, target, send_sem, recv_sem, device):
        copy = pltpu.make_async_remote_copy(
            src_ref=source, dst_ref=target, send_sem=send_sem, recv_sem=recv_sem,
            device_id=device, device_id_type=MESH,
        )
        copy.start()
        sends.append(copy.wait_send)

    def landed(target, sem):
        pltpu.make_async_copy(target, target, sem).wait()

    A, B = pl.ds(0, 4), pl.ds(4, 4)

    def multiply(phase, g):
        if phase == 0:
            vector = start[g]
        else:
            landed(gathered.at[phase - 1, g, pl.ds(0, 7)], g_recv.at[phase - 1, g])
            vector = gathered[phase - 1, g]
        high, low = split(factors(phase, vector))
        mh, ml = (density_high, density_low) if phase == 1 else (fock_high, fock_low)
        box = chunks.at[phase, g]

        def one(slot, ahead):
            rows = pl.ds(pl.multiple_of(lax.rem(x + ahead, 4) * COLS, COLS), COLS)
            box[slot] = times(high, low, mh[rows, :], ml[rows, :]).reshape(PIECES, DEPTH, COLS)

        return box, one

    def x_ends(phase, g):
        s, r = x_send.at[phase, g], x_recv.at[phase, g]
        return s, r

    def stage_x(phase, g):
        box, one = multiply(phase, g)
        s, r = x_ends(phase, g)
        one(0, 2)
        if phase == 0 and g == 0:
            pl.semaphore_wait(barrier, 17 - at_home.astype(jnp.int32))

        send(box.at[0, A], relay_a.at[phase, g], s.at[0], r.at[0], (row, right))
        send(box.at[0, B], relay_b.at[phase, g], s.at[1], r.at[1], (row, left))
        one(1, 1)
        send(box.at[1, B], from_left.at[phase, g, B], s.at[2], r.at[2], (row, right))
        one(2, 3)
        send(box.at[2, A], from_right.at[phase, g, A], s.at[3], r.at[3], (row, left))
        one(3, 0)

    def stage_relay(phase, g):
        box = chunks.at[phase, g]
        s, r = x_ends(phase, g)
        landed(relay_a.at[phase, g], r.at[0])
        box[1, 0:4] = box[1, 0:4] + relay_a[phase, g]
        send(box.at[1, A], from_left.at[phase, g, A], s.at[4], r.at[4], (row, right))
        landed(relay_b.at[phase, g], r.at[1])
        box[2, 4:8] = box[2, 4:8] + relay_b[phase, g]
        send(box.at[2, B], from_right.at[phase, g, B], s.at[5], r.at[5], (row, left))

    def stage_z(phase, g):
        s, r = x_ends(phase, g)
        landed(from_left.at[phase, g, B], r.at[2])
        landed(from_right.at[phase, g, A], r.at[3])
        landed(from_left.at[phase, g, A], r.at[4])
        landed(from_right.at[phase, g, B], r.at[5])
        summed[phase, g] = chunks[phase, g, 3] + from_left[phase, g] + from_right[phase, g]
        s, r = z_send.at[phase, g], z_recv.at[phase, g]
        for j in range(PIECES - 1, 0, -1):
            p = lax.rem(row + j, PIECES)
            send(summed.at[phase, g, p], arrived.at[phase, g, z], s.at[j], r, (p, home))
        copy = pltpu.make_async_remote_copy(
            src_ref=summed.at[phase, g, row], dst_ref=arrived.at[phase, g, z], send_sem=s.at[0], recv_sem=r,
            device_id=(row, home), device_id_type=MESH,
        )

        @pl.when(jnp.logical_not(at_home))
        def _():
            copy.start()

        @pl.when(at_home)
        def _():
            arrived[phase, g, z] = summed[phase, g, row]

        def wait_send():
            @pl.when(jnp.logical_not(at_home))
            def _():
                copy.wait_send()

        sends.append(wait_send)

    def stage_gather(phase, g):
        @pl.when(at_home)
        def _():
            landed(arrived.at[phase, g, pl.ds(0, 7)], z_recv.at[phase, g])

        @pl.when(jnp.logical_not(at_home))
        def _():
            landed(arrived.at[phase, g], z_recv.at[phase, g])

        a = arrived.at[phase, g]
        total = ((a[0] + a[1]) + (a[2] + a[3])) + ((a[4] + a[5]) + (a[6] + a[7]))
        if phase == 0:
            total = total + start[g, row]
        if phase == 2:
            total = total + gathered[1, g, row]
        mine = gathered.at[phase, g, row]
        mine[...] = total
        for j in range(1, PIECES):
            send(mine, mine, g_send.at[phase, g, j], g_recv.at[phase, g], (lax.rem(row + j, PIECES), col))

    for phase in range(3):
        for g in range(GROUPS):
            stage_x(phase, g)
        for g in range(GROUPS):
            stage_relay(phase, g)
        if phase == 0:
            loads[2].wait()
            prepare(density, density_high, density_low)
        for g in range(GROUPS):
            stage_z(phase, g)
        for g in range(GROUPS):
            stage_gather(phase, g)

    parts = []
    for g in range(GROUPS):
        landed(gathered.at[2, g, pl.ds(0, 7)], g_recv.at[2, g])
        parts.append(gathered[2, g])
    for j in range(2):
        turned = [part[:, j * 8 : (j + 1) * 8].reshape(PIECES * 8, COLS) for part in parts]
        out[j] = jnp.concatenate(turned, axis=0).T
    for wait_send in sends:
        wait_send()


def step(fock, density, probe):
    f32, bf16 = jnp.float32, jnp.bfloat16
    vmem, dma = pltpu.VMEM, pltpu.SemaphoreType.DMA
    each = (3, GROUPS)
    return pl.pallas_call(
        kernel,
        out_shape=jax.ShapeDtypeStruct(probe.shape, f32),
        in_specs=[pl.BlockSpec(memory_space=pl.ANY)] * 3,
        out_specs=pl.BlockSpec(memory_space=pltpu.VMEM),
        scratch_shapes=[
            vmem(fock.shape, f32), vmem(density.shape, f32), vmem(probe.shape, f32),
            vmem((ROWS, 2 * COLS), bf16), vmem((ROWS, 2 * COLS), bf16),
            vmem((ROWS, 2 * COLS), bf16), vmem((ROWS, 2 * COLS), bf16),
            vmem((GROUPS, PIECES, DEPTH, COLS), f32),
            vmem((*each, 4, PIECES, DEPTH, COLS), f32),
            vmem((*each, 4, DEPTH, COLS), f32), vmem((*each, 4, DEPTH, COLS), f32),
            vmem((*each, PIECES, DEPTH, COLS), f32), vmem((*each, PIECES, DEPTH, COLS), f32),
            vmem((*each, PIECES, DEPTH, COLS), f32), vmem((*each, 8, DEPTH, COLS), f32),
            vmem((*each, PIECES, DEPTH, COLS), f32),
            dma((3,)), dma((*each, 6)), dma((*each, 6)), dma((*each, PIECES)), dma(each),
            dma((*each, PIECES)), dma(each),
        ],
        compiler_params=pltpu.CompilerParams(
            collective_id=0, has_side_effects=True, vmem_limit_bytes=40 * 1024 * 1024
        ),
    )(fock, density, probe)


def solution(mesh):
    return jax.shard_map(
        step,
        mesh=mesh,
        in_specs=(P(None, "row", "col"), P(None, "row", "col"), P(None, "col", None)),
        out_specs=P(None, "col", None),
        check_vma=False,
    )
```

time: 247 us -> 111 us (0.45)
  blocking collectives: 146 us -> 0 us
  Pallas kernels: 0 us -> 106 us
  waiting for transfers between devices: 53.9 us -> 0 us
  matrix products: 15 us -> 0 us
  between operations: 13.7 us -> 0.01 us
  starting transfers between devices: 6.47 us -> 0 us
  other arithmetic: 6.37 us -> 0 us
    all_to_all x4 -> x0, blocking collectives: 146 us -> none  [the longest x2 74 us: sum_at_owner(): lax.all_to_all(pieces, axis, split_axis=0, concat_axis=0, tiled=True)]
    pallas_call x0 -> x1, Pallas kernels: none -> 106 us  [step(): pl.pallas_call(kernel, out_shape=jax.ShapeDtypeStruct(probe.shape, f32),...]
    all_gather x2 -> x0, waiting for transfers between devices: 28.6 us -> none  [picked(): lax.all_gather(x, axis)]
    all_to_all x1 -> x0, waiting for transfers between devices: 25.3 us -> none  [from_everyone(): return lax.all_to_all(copies, axis, split_axis=0, concat_axis=0, tiled=True)]
    dot_general x9 -> x0, matrix products: 15 us -> none  [the longest x6 11.8 us: plain_dot(): jnp.dot(left, right, precision=lax.Precision.HIGHEST, preferred_element_t...]
    all_to_all x1 -> x0, starting transfers between devices: 6.38 us -> none  [from_everyone(): return lax.all_to_all(copies, axis, split_axis=0, concat_axis=0, tiled=True)]
    unnamed x6 -> x7, local copies, waits for them, and re-layouts: 0.01 us -> 4.84 us
    add x2 -> x0, other arithmetic: 2.81 us -> none  [the longest x1 1.69 us: shards(): result = column_sum + to_columns(row_sum)]
  transfers between devices with their start and end apart: 3 -> 0, of which waited for: 2 -> 0; matrix products, arithmetic and copies ran while one was open for 2% -> 0% of each run, Pallas kernels for 0% -> 0%
where the time goes in v1:
time: 111 us
  Pallas kernels  106 us (95%)
  local copies, waits for them, and re-layouts  4.84 us (4%)
    pallas_call x1, Pallas kernels, step(): pl.pallas_call(kernel, out_shape=jax.ShapeDtypeStruct(probe.shape, f32),...  106 us
    unnamed x7, local copies, waits for them, and re-layouts  4.84 us

profile of v1, /device:TPU:1, one launch (start us, length us, event | category | flops | bytes accessed | tf_op | source)
XLA Modules:
  0.0 111.3 jit_solution(1596698895330861184)
XLA Ops:
  0.0 0.0 copy-start
  0.0 1.6 %copy-done = f32[2,1024,256]{2,1,0:T(8,128)S(1)} copy-done((f32[2,1024,256]{2,1,0:T(8,128)S(1)}, f32[2,1024,256]{2,1,0:T(8,128)}, u32[]{:S(2)}) %copy-start) | copy-done | bytes 2097176
  1.6 0.0 copy-start.1
  1.6 1.6 %copy-done.1 = f32[2,1024,256]{2,1,0:T(8,128)S(1)} copy-done((f32[2,1024,256]{2,1,0:T(8,128)S(1)}, f32[2,1024,256]{2,1,0:T(8,128)}, u32[]{:S(2)}) %copy-start.1) | copy-done | bytes 2097176
  3.2 0.0 copy-start.2
  3.2 0.9 copy-done.2
  4.1 106.4 %shard_map.37 = f32[2,256,128]{2,1,0:T(8,128)S(1)} custom-call(f32[2,1024,256]{2,1,0:T(8,128)S(1)} %copy-done, f32[2,1024,256]{2,1,0:T(8,128)S(1)} %copy-done.1, f32[2,256,128]{2,1,0:T(8,128)S(1)} %copy-done.2), custom_call_target="tpu_custom_call" | custom-call | tf_op jit(solution)/shard_map/pallas_call | solution.py:242
  110.6 0.7 copy.5
Async XLA Ops:
  0.0 1.6 %copy-start = (f32[2,1024,256]{2,1,0:T(8,128)S(1)}, f32[2,1024,256]{2,1,0:T(8,128)}, u32[]{:S(2)}) copy-start(f32[2,1024,256]{2,1,0:T(8,128)} %fock_hbm.1) | copy-start | bytes 6291460
  1.6 1.6 %copy-start.1 = (f32[2,1024,256]{2,1,0:T(8,128)S(1)}, f32[2,1024,256]{2,1,0:T(8,128)}, u32[]{:S(2)}) copy-start(f32[2,1024,256]{2,1,0:T(8,128)} %density_hbm.1) | copy-start | bytes 6291460
  3.2 0.9 copy-start.2

commit v2 on v1

--- a/solution.py
+++ b/solution.py
@@ -58,15 +58,20 @@
 def kernel(
     fock_hbm, density_hbm, probe_hbm, out,
     fock, density, probe, fock_high, fock_low, density_high, density_low,
-    start, chunks, relay_a, relay_b, from_left, from_right, summed, arrived, gathered,
-    load_sem, x_send, x_recv, z_send, z_recv, g_send, g_recv,
+    start, chunks, relay_a, relay_b, from_left, from_right, summed, turned, arrived, gathered,
+    load_sem, x_send, x_recv, y_send, y_recv, z_send, z_recv, g_send, g_recv,
 ):
     row, col = lax.axis_index("row"), lax.axis_index("col")
     z, x = col // 4, lax.rem(col, 4)
     right = z * 4 + lax.rem(x + 1, 4)
     left = z * 4 + lax.rem(x + 3, 4)
-    home = row * 4 + x
-    at_home = row == z
+    y, core = row // 2, lax.rem(row, 2)
+
+    def peer(dy, dc):
+        return lax.rem(y + dy, 4) * 2 + lax.rem(core + dc, 2)
+
+    peers = [peer(*d) for d in ((2, 0), (2, 1), (1, 0), (3, 0), (1, 1), (3, 1), (0, 1))]
+    from_peers = [peer(*d) for d in ((0, 1), (1, 0), (3, 0), (1, 1), (3, 1), (2, 0), (2, 1))]
 
     loads = [
         pltpu.make_async_copy(source, target, load_sem.at[i])
@@ -86,17 +91,13 @@
     hello(row, left)
     for j in range(1, PIECES):
         hello(lax.rem(row + j, PIECES), col)
-        hello(z, lax.rem(z + j, 8) * 4 + x)
-
-    @pl.when(jnp.logical_not(at_home))
-    def _():
-        hello(z, col)
+        hello(row, lax.rem(z + j, 8) * 4 + x)
 
     loads[0].wait()
     for j in range(2):
-        turned = probe[j].T
-        for g in range(GROUPS):
-            start[g, :, j * 8 : (j + 1) * 8, :] = turned[g * 64 : (g + 1) * 64].reshape(PIECES, 8, COLS)
+        probe_t = probe[j].T
+        for g in range(GROUPS):
+            start[g, :, j * 8 : (j + 1) * 8, :] = probe_t[g * 64 : (g + 1) * 64].reshape(PIECES, 8, COLS)
     loads[1].wait()
     prepare(fock, fock_high, fock_low)
 
@@ -110,8 +111,11 @@
         copy.start()
         sends.append(copy.wait_send)
 
+    def landing(target, sem):
+        return pltpu.make_async_copy(target, target, sem).wait
+
     def landed(target, sem):
-        pltpu.make_async_copy(target, target, sem).wait()
+        landing(target, sem)()
 
     A, B = pl.ds(0, 4), pl.ds(4, 4)
 
@@ -140,7 +144,7 @@
         s, r = x_ends(phase, g)
         one(0, 2)
         if phase == 0 and g == 0:
-            pl.semaphore_wait(barrier, 17 - at_home.astype(jnp.int32))
+            pl.semaphore_wait(barrier, 16)
 
         send(box.at[0, A], relay_a.at[phase, g], s.at[0], r.at[0], (row, right))
         send(box.at[0, B], relay_b.at[phase, g], s.at[1], r.at[1], (row, left))
@@ -160,47 +164,42 @@
         box[2, 4:8] = box[2, 4:8] + relay_b[phase, g]
         send(box.at[2, B], from_right.at[phase, g, B], s.at[5], r.at[5], (row, left))
 
-    def stage_z(phase, g):
+    def stage_y(phase, g):
         s, r = x_ends(phase, g)
         landed(from_left.at[phase, g, B], r.at[2])
         landed(from_right.at[phase, g, A], r.at[3])
         landed(from_left.at[phase, g, A], r.at[4])
         landed(from_right.at[phase, g, B], r.at[5])
         summed[phase, g] = chunks[phase, g, 3] + from_left[phase, g] + from_right[phase, g]
-        s, r = z_send.at[phase, g], z_recv.at[phase, g]
-        for j in range(PIECES - 1, 0, -1):
-            p = lax.rem(row + j, PIECES)
-            send(summed.at[phase, g, p], arrived.at[phase, g, z], s.at[j], r, (p, home))
-        copy = pltpu.make_async_remote_copy(
-            src_ref=summed.at[phase, g, row], dst_ref=arrived.at[phase, g, z], send_sem=s.at[0], recv_sem=r,
-            device_id=(row, home), device_id_type=MESH,
-        )
-
-        @pl.when(jnp.logical_not(at_home))
+        s, r = y_send.at[phase, g], y_recv.at[phase, g]
+        for p in peers:
+            send(summed.at[phase, g, p], turned.at[phase, g, row], s.at[p], r.at[row], (p, col))
+        along_z(phase, g, row, summed.at[phase, g, row])
+
+    def along_z(phase, g, block, source):
+        @pl.when(block != z)
         def _():
-            copy.start()
-
-        @pl.when(at_home)
+            pltpu.make_async_remote_copy(
+                src_ref=source, dst_ref=arrived.at[phase, g, z],
+                send_sem=z_send.at[phase, g, block], recv_sem=z_recv.at[phase, g],
+                device_id=(row, block * 4 + x), device_id_type=MESH,
+            ).start()
+
+        @pl.when(block == z)
         def _():
-            arrived[phase, g, z] = summed[phase, g, row]
-
-        def wait_send():
-            @pl.when(jnp.logical_not(at_home))
-            def _():
-                copy.wait_send()
-
-        sends.append(wait_send)
+            arrived[phase, g, z] = source[...]
+
+    def stage_z(phase, g):
+        for p in from_peers:
+            piece = turned.at[phase, g, p]
+            landed(piece, y_recv.at[phase, g, p])
+            along_z(phase, g, p, piece)
+        for j in range(1, 8):
+            sends.append(landing(arrived.at[phase, g, 0], z_send.at[phase, g, lax.rem(z + j, 8)]))
 
     def stage_gather(phase, g):
-        @pl.when(at_home)
-        def _():
-            landed(arrived.at[phase, g, pl.ds(0, 7)], z_recv.at[phase, g])
-
-        @pl.when(jnp.logical_not(at_home))
-        def _():
-            landed(arrived.at[phase, g], z_recv.at[phase, g])
-
         a = arrived.at[phase, g]
+        landed(arrived.at[phase, g, pl.ds(0, 7)], z_recv.at[phase, g])
         total = ((a[0] + a[1]) + (a[2] + a[3])) + ((a[4] + a[5]) + (a[6] + a[7]))
         if phase == 0:
             total = total + start[g, row]
@@ -208,8 +207,8 @@
             total = total + gathered[1, g, row]
         mine = gathered.at[phase, g, row]
         mine[...] = total
-        for j in range(1, PIECES):
-            send(mine, mine, g_send.at[phase, g, j], g_recv.at[phase, g], (lax.rem(row + j, PIECES), col))
+        for p in peers:
+            send(mine, mine, g_send.at[phase, g, p], g_recv.at[phase, g], (p, col))
 
     for phase in range(3):
         for g in range(GROUPS):
@@ -219,6 +218,8 @@
         if phase == 0:
             loads[2].wait()
             prepare(density, density_high, density_low)
+        for g in range(GROUPS):
+            stage_y(phase, g)
         for g in range(GROUPS):
             stage_z(phase, g)
         for g in range(GROUPS):
@@ -229,8 +230,8 @@
         landed(gathered.at[2, g, pl.ds(0, 7)], g_recv.at[2, g])
         parts.append(gathered[2, g])
     for j in range(2):
-        turned = [part[:, j * 8 : (j + 1) * 8].reshape(PIECES * 8, COLS) for part in parts]
-        out[j] = jnp.concatenate(turned, axis=0).T
+        halves = [part[:, j * 8 : (j + 1) * 8].reshape(PIECES * 8, COLS) for part in parts]
+        out[j] = jnp.concatenate(halves, axis=0).T
     for wait_send in sends:
         wait_send()
 
@@ -252,9 +253,11 @@
             vmem((*each, 4, PIECES, DEPTH, COLS), f32),
             vmem((*each, 4, DEPTH, COLS), f32), vmem((*each, 4, DEPTH, COLS), f32),
             vmem((*each, PIECES, DEPTH, COLS), f32), vmem((*each, PIECES, DEPTH, COLS), f32),
-            vmem((*each, PIECES, DEPTH, COLS), f32), vmem((*each, 8, DEPTH, COLS), f32),
+            vmem((*each, PIECES, DEPTH, COLS), f32), vmem((*each, PIECES, DEPTH, COLS), f32),
+            vmem((*each, 8, DEPTH, COLS), f32),
             vmem((*each, PIECES, DEPTH, COLS), f32),
-            dma((3,)), dma((*each, 6)), dma((*each, 6)), dma((*each, PIECES)), dma(each),
+            dma((3,)), dma((*each, 6)), dma((*each, 6)), dma((*each, PIECES)), dma((*each, PIECES)),
+            dma((*each, 8)), dma(each),
             dma((*each, PIECES)), dma(each),
         ],
         compiler_params=pltpu.CompilerParams(

time: 111 us -> 95.6 us (0.86)
  Pallas kernels: 106 us -> 90.6 us
    pallas_call x1, Pallas kernels: 106 us -> 90.6 us  [step(): pl.pallas_call(kernel, out_shape=jax.ShapeDtypeStruct(probe.shape, f32),...]
where the time goes in v2:
time: 95.6 us; the launch traced here: 95.5 us
  Pallas kernels  90.6 us (95%)
  local copies, waits for them, and re-layouts  4.84 us (5%)
    pallas_call x1, Pallas kernels, step(): pl.pallas_call(kernel, out_shape=jax.ShapeDtypeStruct(probe.shape, f32),...  90.6 us
    unnamed x7, local copies, waits for them, and re-layouts  4.84 us

profile of v2, /device:TPU:1, one launch (start us, length us, event | category | flops | bytes accessed | tf_op | source)
XLA Modules:
  0.0 95.5 jit_solution(2792052299132394141)
XLA Ops:
  0.0 0.0 copy-start
  0.0 1.6 %copy-done = f32[2,1024,256]{2,1,0:T(8,128)S(1)} copy-done((f32[2,1024,256]{2,1,0:T(8,128)S(1)}, f32[2,1024,256]{2,1,0:T(8,128)}, u32[]{:S(2)}) %copy-start) | copy-done | bytes 2097176
  1.6 0.0 copy-start.1
  1.6 1.6 %copy-done.1 = f32[2,1024,256]{2,1,0:T(8,128)S(1)} copy-done((f32[2,1024,256]{2,1,0:T(8,128)S(1)}, f32[2,1024,256]{2,1,0:T(8,128)}, u32[]{:S(2)}) %copy-start.1) | copy-done | bytes 2097176
  3.2 0.0 copy-start.2
  3.2 0.9 copy-done.2
  4.1 90.6 %shard_map.37 = f32[2,256,128]{2,1,0:T(8,128)S(1)} custom-call(f32[2,1024,256]{2,1,0:T(8,128)S(1)} %copy-done, f32[2,1024,256]{2,1,0:T(8,128)S(1)} %copy-done.1, f32[2,256,128]{2,1,0:T(8,128)S(1)} %copy-done.2), custom_call_target="tpu_custom_call" | custom-call | tf_op jit(solution)/shard_map/pallas_call | solution.py:243
  94.8 0.7 copy.5
Async XLA Ops:
  0.0 1.6 %copy-start = (f32[2,1024,256]{2,1,0:T(8,128)S(1)}, f32[2,1024,256]{2,1,0:T(8,128)}, u32[]{:S(2)}) copy-start(f32[2,1024,256]{2,1,0:T(8,128)} %fock_hbm.1) | copy-start | bytes 6291460
  1.6 1.6 %copy-start.1 = (f32[2,1024,256]{2,1,0:T(8,128)S(1)}, f32[2,1024,256]{2,1,0:T(8,128)}, u32[]{:S(2)}) copy-start(f32[2,1024,256]{2,1,0:T(8,128)} %density_hbm.1) | copy-start | bytes 6291460
  3.2 0.9 copy-start.2

commit v3 on v2

--- a/solution.py
+++ b/solution.py
@@ -9,12 +9,29 @@
 
 MESH = pl.DeviceIdType.MESH
 DT = 0.5
-GROUPS = 2
 ROWS = 1024
 COLS = 256
 PIECES = 8
 DEPTH = 16
-WIDE = PIECES * DEPTH
+GROUPS = 2
+CUTS = GROUPS // 2
+WIDE = COLS // CUTS
+KINDS = PIECES // CUTS
+TALL = KINDS * DEPTH
+PHASES = 3
+TIMES = {"x": 0.0, "relay": 3.1, "y": 6.2, "z": 10.0, "gather": 16.0}
+PERIOD = 21.0
+APART = 4.2
+
+
+def timetable():
+    turns = [
+        (phase * PERIOD + g * APART + at, phase, g, name)
+        for phase in range(PHASES)
+        for g in range(GROUPS)
+        for name, at in TIMES.items()
+    ]
+    return [turn[1:] for turn in sorted(turns, key=lambda turn: turn[0])]
 
 
 def split(value):
@@ -34,6 +51,11 @@
     lax.fori_loop(0, ROWS // COLS, part, 0)
 
 
+def flat(vector):
+    parts = [vector[i * KINDS : (i + 1) * KINDS].reshape(TALL, WIDE) for i in range(CUTS)]
+    return jnp.concatenate(parts, axis=1) if CUTS > 1 else parts[0]
+
+
 def factors(phase, vector):
     real, imag = vector[:, :8], vector[:, 8:]
     if phase == 1:
@@ -41,8 +63,8 @@
     else:
         dt = DT if phase == 0 else -DT
         first, second = (-dt * imag, dt * real), (-dt * real, -dt * imag)
-    first = jnp.concatenate(first, axis=1).reshape(WIDE, COLS)
-    second = jnp.concatenate(second, axis=1).reshape(WIDE, COLS)
+    first = flat(jnp.concatenate(first, axis=1))
+    second = flat(jnp.concatenate(second, axis=1))
     return jnp.concatenate([first, second], axis=1)
 
 
@@ -52,7 +74,8 @@
         dimension_numbers=(((1,), (1,)), ((), ())),
         preferred_element_type=jnp.float32,
     )
-    return dot(high, matrix_high) + (dot(low, matrix_high) + dot(high, matrix_low))
+    both = dot(jnp.concatenate([high, low], axis=0), matrix_high)
+    return both[:TALL] + (both[TALL:] + dot(high, matrix_low))
 
 
 def kernel(
@@ -87,17 +110,18 @@
     def hello(r, c):
         pl.semaphore_signal(barrier, inc=1, device_id=(r, c), device_id_type=MESH)
 
+    for j in range(1, 8):
+        hello(row, lax.rem(z + j, 8) * 4 + x)
+    for p in peers:
+        hello(p, col)
     hello(row, right)
     hello(row, left)
-    for j in range(1, PIECES):
-        hello(lax.rem(row + j, PIECES), col)
-        hello(row, lax.rem(z + j, 8) * 4 + x)
 
     loads[0].wait()
     for j in range(2):
-        probe_t = probe[j].T
-        for g in range(GROUPS):
-            start[g, :, j * 8 : (j + 1) * 8, :] = probe_t[g * 64 : (g + 1) * 64].reshape(PIECES, 8, COLS)
+        probe_t = probe[j].T.reshape(GROUPS, KINDS, 8, COLS)
+        for i in range(CUTS):
+            start[:, i * KINDS : (i + 1) * KINDS, j * 8 : (j + 1) * 8, :] = probe_t[..., i * WIDE : (i + 1) * WIDE]
     loads[1].wait()
     prepare(fock, fock_high, fock_low)
 
@@ -119,7 +143,7 @@
 
     A, B = pl.ds(0, 4), pl.ds(4, 4)
 
-    def multiply(phase, g):
+    def stage_x(phase, g):
         if phase == 0:
             vector = start[g]
         else:
@@ -128,24 +152,17 @@
         high, low = split(factors(phase, vector))
         mh, ml = (density_high, density_low) if phase == 1 else (fock_high, fock_low)
         box = chunks.at[phase, g]
+        s, r = x_send.at[phase, g], x_recv.at[phase, g]
 
         def one(slot, ahead):
             rows = pl.ds(pl.multiple_of(lax.rem(x + ahead, 4) * COLS, COLS), COLS)
-            box[slot] = times(high, low, mh[rows, :], ml[rows, :]).reshape(PIECES, DEPTH, COLS)
-
-        return box, one
-
-    def x_ends(phase, g):
-        s, r = x_send.at[phase, g], x_recv.at[phase, g]
-        return s, r
-
-    def stage_x(phase, g):
-        box, one = multiply(phase, g)
-        s, r = x_ends(phase, g)
+            value = times(high, low, mh[rows, :], ml[rows, :])
+            for i in range(CUTS):
+                box[slot, i * KINDS : (i + 1) * KINDS] = value[:, i * WIDE : (i + 1) * WIDE].reshape(KINDS, DEPTH, WIDE)
+
         one(0, 2)
         if phase == 0 and g == 0:
             pl.semaphore_wait(barrier, 16)
-
         send(box.at[0, A], relay_a.at[phase, g], s.at[0], r.at[0], (row, right))
         send(box.at[0, B], relay_b.at[phase, g], s.at[1], r.at[1], (row, left))
         one(1, 1)
@@ -156,7 +173,7 @@
 
     def stage_relay(phase, g):
         box = chunks.at[phase, g]
-        s, r = x_ends(phase, g)
+        s, r = x_send.at[phase, g], x_recv.at[phase, g]
         landed(relay_a.at[phase, g], r.at[0])
         box[1, 0:4] = box[1, 0:4] + relay_a[phase, g]
         send(box.at[1, A], from_left.at[phase, g, A], s.at[4], r.at[4], (row, right))
@@ -165,7 +182,7 @@
         send(box.at[2, B], from_right.at[phase, g, B], s.at[5], r.at[5], (row, left))
 
     def stage_y(phase, g):
-        s, r = x_ends(phase, g)
+        r = x_recv.at[phase, g]
         landed(from_left.at[phase, g, B], r.at[2])
         landed(from_right.at[phase, g, A], r.at[3])
         landed(from_left.at[phase, g, A], r.at[4])
@@ -174,6 +191,7 @@
         s, r = y_send.at[phase, g], y_recv.at[phase, g]
         for p in peers:
             send(summed.at[phase, g, p], turned.at[phase, g, row], s.at[p], r.at[row], (p, col))
+        turned[phase, g, row] = summed[phase, g, row]
         along_z(phase, g, row, summed.at[phase, g, row])
 
     def along_z(phase, g, block, source):
@@ -185,15 +203,12 @@
                 device_id=(row, block * 4 + x), device_id_type=MESH,
             ).start()
 
-        @pl.when(block == z)
-        def _():
-            arrived[phase, g, z] = source[...]
-
     def stage_z(phase, g):
         for p in from_peers:
             piece = turned.at[phase, g, p]
             landed(piece, y_recv.at[phase, g, p])
             along_z(phase, g, p, piece)
+        arrived[phase, g, z] = turned[phase, g, z]
         for j in range(1, 8):
             sends.append(landing(arrived.at[phase, g, 0], z_send.at[phase, g, lax.rem(z + j, 8)]))
 
@@ -210,27 +225,25 @@
         for p in peers:
             send(mine, mine, g_send.at[phase, g, p], g_recv.at[phase, g], (p, col))
 
-    for phase in range(3):
-        for g in range(GROUPS):
-            stage_x(phase, g)
-        for g in range(GROUPS):
-            stage_relay(phase, g)
-        if phase == 0:
+    stages = {"x": stage_x, "relay": stage_relay, "y": stage_y, "z": stage_z, "gather": stage_gather}
+    ready = False
+    for phase, g, name in timetable():
+        if phase == 0 and name == "y" and not ready:
+            ready = True
             loads[2].wait()
             prepare(density, density_high, density_low)
-        for g in range(GROUPS):
-            stage_y(phase, g)
-        for g in range(GROUPS):
-            stage_z(phase, g)
-        for g in range(GROUPS):
-            stage_gather(phase, g)
+        stages[name](phase, g)
 
     parts = []
     for g in range(GROUPS):
         landed(gathered.at[2, g, pl.ds(0, 7)], g_recv.at[2, g])
         parts.append(gathered[2, g])
     for j in range(2):
-        halves = [part[:, j * 8 : (j + 1) * 8].reshape(PIECES * 8, COLS) for part in parts]
+        halves = []
+        for part in parts:
+            half = part[:, j * 8 : (j + 1) * 8]
+            cuts = [half[i * KINDS : (i + 1) * KINDS].reshape(KINDS * 8, WIDE) for i in range(CUTS)]
+            halves.append(jnp.concatenate(cuts, axis=1) if CUTS > 1 else cuts[0])
         out[j] = jnp.concatenate(halves, axis=0).T
     for wait_send in sends:
         wait_send()
@@ -239,29 +252,28 @@
 def step(fock, density, probe):
     f32, bf16 = jnp.float32, jnp.bfloat16
     vmem, dma = pltpu.VMEM, pltpu.SemaphoreType.DMA
-    each = (3, GROUPS)
+    each = (PHASES, GROUPS)
+    piece = (DEPTH, WIDE)
     return pl.pallas_call(
         kernel,
         out_shape=jax.ShapeDtypeStruct(probe.shape, f32),
-        in_specs=[pl.BlockSpec(memory_space=pl.ANY)] * 3,
+        in_specs=[pl.BlockSpec(memory_space=pltpu.HBM)] * 3,
         out_specs=pl.BlockSpec(memory_space=pltpu.VMEM),
         scratch_shapes=[
             vmem(fock.shape, f32), vmem(density.shape, f32), vmem(probe.shape, f32),
             vmem((ROWS, 2 * COLS), bf16), vmem((ROWS, 2 * COLS), bf16),
             vmem((ROWS, 2 * COLS), bf16), vmem((ROWS, 2 * COLS), bf16),
-            vmem((GROUPS, PIECES, DEPTH, COLS), f32),
-            vmem((*each, 4, PIECES, DEPTH, COLS), f32),
-            vmem((*each, 4, DEPTH, COLS), f32), vmem((*each, 4, DEPTH, COLS), f32),
-            vmem((*each, PIECES, DEPTH, COLS), f32), vmem((*each, PIECES, DEPTH, COLS), f32),
-            vmem((*each, PIECES, DEPTH, COLS), f32), vmem((*each, PIECES, DEPTH, COLS), f32),
-            vmem((*each, 8, DEPTH, COLS), f32),
-            vmem((*each, PIECES, DEPTH, COLS), f32),
+            vmem((GROUPS, PIECES, *piece), f32),
+            vmem((*each, 4, PIECES, *piece), f32),
+            vmem((*each, 4, *piece), f32), vmem((*each, 4, *piece), f32),
+            vmem((*each, PIECES, *piece), f32), vmem((*each, PIECES, *piece), f32),
+            vmem((*each, PIECES, *piece), f32), vmem((*each, PIECES, *piece), f32),
+            vmem((*each, 8, *piece), f32), vmem((*each, PIECES, *piece), f32),
             dma((3,)), dma((*each, 6)), dma((*each, 6)), dma((*each, PIECES)), dma((*each, PIECES)),
-            dma((*each, 8)), dma(each),
-            dma((*each, PIECES)), dma(each),
+            dma((*each, 8)), dma(each), dma((*each, PIECES)), dma(each),
         ],
         compiler_params=pltpu.CompilerParams(
-            collective_id=0, has_side_effects=True, vmem_limit_bytes=40 * 1024 * 1024
+            collective_id=0, has_side_effects=True, vmem_limit_bytes=60 * 1024 * 1024
         ),
     )(fock, density, probe)
 

time: 95.6 us -> 85.5 us (0.89)
  Pallas kernels: 90.6 us -> 83.7 us
  local copies, waits for them, and re-layouts: 4.84 us -> 1.67 us
    pallas_call x1, Pallas kernels: 90.6 us -> 83.7 us  [step(): pl.pallas_call(kernel, out_shape=jax.ShapeDtypeStruct(probe.shape, f32),...]
    unnamed x7 -> x1, local copies, waits for them, and re-layouts: 4.84 us -> 1.67 us
where the time goes in v3:
time: 85.5 us; the launch traced here: 85.4 us
  Pallas kernels  83.7 us (98%)
  local copies, waits for them, and re-layouts  1.67 us (2%)
    pallas_call x1, Pallas kernels, step(): pl.pallas_call(kernel, out_shape=jax.ShapeDtypeStruct(probe.shape, f32),...  83.7 us

profile of v3, /device:TPU:1, one launch (start us, length us, event | category | flops | bytes accessed | tf_op | source)
XLA Modules:
  0.0 85.4 jit_solution(13391568337167990550)
XLA Ops:
  0.0 83.7 %shard_map.37 = f32[2,256,128]{2,1,0:T(8,128)} custom-call(f32[2,1024,256]{2,1,0:T(8,128)} %fock_hbm.1, f32[2,1024,256]{2,1,0:T(8,128)} %density_hbm.1, f32[2,256,128]{2,1,0:T(8,128)} %probe_hbm.1), custom_call_target="tpu_custom_call" | custom-call | tf_op jit(solution)/shard_map/pallas_call | solution.py:257
  83.7 1.7 %copy.5 = f32[2,256,128]{2,1,0:T(8,128)} copy(f32[2,256,128]{2,1,0:T(8,128)} %shard_map.37) | data formatting | bytes 524288

commit v4 on v3

v4 whole, which is shorter than its diff:
```python
import functools

import jax
import jax.numpy as jnp
from jax import lax
from jax.experimental import pallas as pl
from jax.experimental.pallas import tpu as pltpu
from jax.sharding import PartitionSpec as P

MESH = pl.DeviceIdType.MESH
DT = 0.5
ROWS = 1024
COLS = 256
PIECES = 8
DEPTH = 16
GROUPS = 2
CUTS = GROUPS // 2
WIDE = COLS // CUTS
KINDS = PIECES // CUTS
TALL = KINDS * DEPTH
PHASES = 3
VMEM_LIMIT = 60 * 1024 * 1024
APART = 4.2


def split(value):
    high = value.astype(jnp.bfloat16)
    return high, (value - high.astype(jnp.float32)).astype(jnp.bfloat16)


def flat(vector):
    parts = [vector[i * KINDS : (i + 1) * KINDS].reshape(TALL, WIDE) for i in range(CUTS)]
    return jnp.concatenate(parts, axis=1) if CUTS > 1 else parts[0]


def factors(phase, vector):
    real, imag = vector[:, :8], vector[:, 8:]
    if phase == 1:
        first, second = (real, imag), (imag, -real)
    else:
        dt = DT if phase == 0 else -DT
        first, second = (-dt * imag, dt * real), (-dt * real, -dt * imag)
    first = flat(jnp.concatenate(first, axis=1))
    second = flat(jnp.concatenate(second, axis=1))
    return split(jnp.concatenate([first, second], axis=1))


def times(high, low, matrix_high, matrix_low, depth_dim):
    dot = functools.partial(
        lax.dot_general,
        dimension_numbers=(((1,), (depth_dim,)), ((), ())),
        preferred_element_type=jnp.float32,
    )
    both = dot(jnp.concatenate([high, low], axis=0), matrix_high)
    return both[:TALL] + (both[TALL:] + dot(high, matrix_low))


def kernel(
    fock_hbm, density_hbm, probe_hbm, out,
    fock, density, probe, fock_high, fock_low, density_high, density_low,
    start, chunks, relay_a, relay_b, from_left, from_right, summed, turned, arrived, blocks, sums, gathered,
    load_sem, x_send, x_recv, y_send, y_recv, z_send, z_recv, g_send, g_recv, zg_send, zg_recv, xg_send, xg_recv,
):
    row, col = lax.axis_index("row"), lax.axis_index("col")
    z, x = col // 4, lax.rem(col, 4)
    y, core = row // 2, lax.rem(row, 2)
    right = (row, z * 4 + lax.rem(x + 1, 4))
    left = (row, z * 4 + lax.rem(x + 3, 4))

    def along_x(ahead):
        return lax.rem(x + ahead, 4)

    def along_z(ahead):
        return lax.rem(z + ahead, 8)

    def peer(dy, dc):
        return lax.rem(y + dy, 4) * 2 + lax.rem(core + dc, 2)

    peers = [peer(*d) for d in ((2, 0), (2, 1), (1, 0), (3, 0), (1, 1), (3, 1), (0, 1))]
    from_peers = [peer(*d) for d in ((0, 1), (1, 0), (3, 0), (1, 1), (3, 1), (2, 0), (2, 1))]
    z_order = (4, 3, 5, 2, 6, 1, 7)

    barrier = pltpu.get_barrier_semaphore()

    def hello(r, c):
        pl.semaphore_signal(barrier, inc=1, device_id=(r, c), device_id_type=MESH)

    for j in z_order:
        hello(row, along_z(j) * 4 + x)
    for p in peers:
        hello(p, col)
    hello(*right)
    hello(*left)

    def rows_of(block):
        return pl.ds(pl.multiple_of(block * COLS, COLS), COLS)

    probe_load = pltpu.make_async_copy(probe_hbm, probe, load_sem.at[0])
    density_load = pltpu.make_async_copy(density_hbm, density, load_sem.at[1])
    fock_loads = {}
    probe_load.start()
    for i, ahead in enumerate((2, 1, 3, 0)):
        rows = rows_of(along_x(ahead))
        fock_loads[ahead] = pltpu.make_async_copy(fock_hbm.at[:, rows, :], fock.at[:, rows, :], load_sem.at[2 + i])
        fock_loads[ahead].start()

    probe_load.wait()
    for j in range(2):
        probe_t = probe[j].T.reshape(GROUPS, KINDS, 8, COLS)
        for i in range(CUTS):
            start[:, i * KINDS : (i + 1) * KINDS, j * 8 : (j + 1) * 8, :] = probe_t[..., i * WIDE : (i + 1) * WIDE]

    sends = []

    def send(source, target, send_sem, recv_sem, device):
        copy = pltpu.make_async_remote_copy(
            src_ref=source, dst_ref=target, send_sem=send_sem, recv_sem=recv_sem,
            device_id=device, device_id_type=MESH,
        )
        copy.start()
        sends.append(copy.wait_send)

    def landing(target, sem):
        return pltpu.make_async_copy(target, target, sem).wait

    def landed(target, sem):
        landing(target, sem)()

    def store(box, value):
        for i in range(CUTS):
            box[i * KINDS : (i + 1) * KINDS] = value[:, i * WIDE : (i + 1) * WIDE].reshape(KINDS, DEPTH, WIDE)

    A, B = pl.ds(0, 4), pl.ds(4, 4)

    def stage_x(phase, g):
        if phase == 0:
            vector = start[g]
        else:
            landed(gathered.at[1, g, pl.ds(0, 7)], g_recv.at[1, g])
            vector = gathered[1, g]
        high, low = factors(phase, vector)
        box = chunks.at[phase, g]
        s, r = x_send.at[phase, g], x_recv.at[phase, g]

        def one(slot, ahead):
            rows = rows_of(along_x(ahead))
            if phase == 0 and g == 0:
                fock_loads[ahead].wait()
                for j in range(2):
                    h, l = split(fock[j, rows, :])
                    fock_high[rows, j * COLS : (j + 1) * COLS] = h
                    fock_low[rows, j * COLS : (j + 1) * COLS] = l
            store(box.at[slot], times(high, low, fock_high[rows, :], fock_low[rows, :], 1))

        one(0, 2)
        if phase == 0 and g == 0:
            pl.semaphore_wait(barrier, 16)
        send(box.at[0, A], relay_a.at[phase, g], s.at[0], r.at[0], right)
        send(box.at[0, B], relay_b.at[phase, g], s.at[1], r.at[1], left)
        one(1, 1)
        send(box.at[1, B], from_left.at[phase, g, B], s.at[2], r.at[2], right)
        one(2, 3)
        send(box.at[2, A], from_right.at[phase, g, A], s.at[3], r.at[3], left)
        one(3, 0)
        if phase == 0:
            if g == 0:
                density_load.start()

            @pl.when(z == row)
            def _():
                box[3] = box[3] + start[g]

    def stage_relay(phase, g):
        box = chunks.at[phase, g]
        s, r = x_send.at[phase, g], x_recv.at[phase, g]
        landed(relay_a.at[phase, g], r.at[0])
        box[1, 0:4] = box[1, 0:4] + relay_a[phase, g]
        send(box.at[1, A], from_left.at[phase, g, A], s.at[4], r.at[4], right)
        landed(relay_b.at[phase, g], r.at[1])
        box[2, 4:8] = box[2, 4:8] + relay_b[phase, g]
        send(box.at[2, B], from_right.at[phase, g, B], s.at[5], r.at[5], left)

    def sum_x(phase, g):
        r = x_recv.at[phase, g]
        landed(from_left.at[phase, g, B], r.at[2])
        landed(from_right.at[phase, g, A], r.at[3])
        landed(from_left.at[phase, g, A], r.at[4])
        landed(from_right.at[phase, g, B], r.at[5])
        summed[phase, g] = chunks[phase, g, 3] + from_left[phase, g] + from_right[phase, g]

    def sum_of(a):
        return ((a[0] + a[1]) + (a[2] + a[3])) + ((a[4] + a[5]) + (a[6] + a[7]))

    def stage_spread(g):
        sum_x(0, g)
        for o in z_order:
            j = along_z(o)
            send(summed.at[0, g, j], arrived.at[0, g, z], z_send.at[0, g, j], z_recv.at[0, g], (row, j * 4 + x))
        arrived[0, g, z] = summed[0, g, z]

    def stage_collect(g):
        landed(arrived.at[0, g, pl.ds(0, 7)], z_recv.at[0, g])
        mine = blocks.at[g, x, z]
        mine[...] = sum_of(arrived.at[0, g])
        for o in z_order:
            j = along_z(o)
            send(mine, mine, zg_send.at[g, j], zg_recv.at[g, z], (row, j * 4 + x))
        forward(g, 0)

    def forward(g, *offsets):
        for o in offsets:
            j = along_z(o)
            piece = blocks.at[g, x, j]
            if o:
                landed(piece, zg_recv.at[g, j])
            send(piece, piece, xg_send.at[g, 0, j], xg_recv.at[g, 0, j], right)
            send(piece, piece, xg_send.at[g, 1, j], xg_recv.at[g, 1, j], left)

    def onward(g, *offsets):
        for o in offsets:
            j = along_z(o)
            back, at, way = (3, 0, right) if o < 4 else (1, 1, left)
            piece = blocks.at[g, along_x(back), j]
            landed(piece, xg_recv.at[g, at, j])
            send(piece, piece, xg_send.at[g, 2, j], xg_recv.at[g, 2, j], way)

    def adjoint(g, ahead):
        block = along_x(ahead)
        high, low = factors(1, blocks[g, block])
        return times(high, low, density_high[block], density_low[block], 0)

    def stage_own(g):
        sums[g] = adjoint(g, 0)

    def stage_next(g):
        for o in range(8):
            j = along_z(o)
            back, at = (1, 1) if o < 4 else (3, 0)
            landed(blocks.at[g, along_x(back), j], xg_recv.at[g, at, j])
        sums[g] = sums[g] + (adjoint(g, 1) + adjoint(g, 3))

    def stage_far(g):
        for o in range(8):
            j = along_z(o)
            landed(blocks.at[g, along_x(2), j], xg_recv.at[g, 2, j])
        store(summed.at[1, g], sums[g] + adjoint(g, 2))
        for p in peers:
            send(summed.at[1, g, p], turned.at[1, g, row], y_send.at[1, g, p], y_recv.at[1, g, 0], (p, col))
        turned[1, g, row] = summed[1, g, row]

    def stage_join(g):
        landed(turned.at[1, g, pl.ds(0, 7)], y_recv.at[1, g, 0])
        gather(1, g, sum_of(turned.at[1, g]))

    def gather(phase, g, value):
        mine = gathered.at[phase, g, row]
        mine[...] = value
        for p in peers:
            send(mine, mine, g_send.at[phase, g, p], g_recv.at[phase, g], (p, col))

    def to_z(g, block, source):
        @pl.when(block != z)
        def _():
            pltpu.make_async_remote_copy(
                src_ref=source, dst_ref=arrived.at[2, g, z],
                send_sem=z_send.at[2, g, block], recv_sem=z_recv.at[2, g],
                device_id=(row, block * 4 + x), device_id_type=MESH,
            ).start()

    def stage_y(g):
        sum_x(2, g)
        for p in peers:
            send(summed.at[2, g, p], turned.at[2, g, row], y_send.at[2, g, p], y_recv.at[2, g, row], (p, col))
        turned[2, g, row] = summed[2, g, row]
        to_z(g, row, summed.at[2, g, row])

    def stage_z(g):
        for p in from_peers:
            piece = turned.at[2, g, p]
            landed(piece, y_recv.at[2, g, p])
            to_z(g, p, piece)
        arrived[2, g, z] = turned[2, g, z]
        for j in range(1, 8):
            sends.append(landing(arrived.at[2, g, 0], z_send.at[2, g, along_z(j)]))

    def stage_gather(g):
        landed(arrived.at[2, g, pl.ds(0, 7)], z_recv.at[2, g])
        gather(2, g, sum_of(arrived.at[2, g]) + gathered[1, g, row])

    def stage_density(g):
        if g == 0:
            density_load.wait()

            def part(i, carry):
                for j in range(2):
                    h, l = split(density[j, rows_of(i), :])
                    density_high[i, j * COLS : (j + 1) * COLS] = h
                    density_low[i, j * COLS : (j + 1) * COLS] = l
                return carry

            lax.fori_loop(0, ROWS // COLS, part, 0)

    def stage_out(g):
        landed(gathered.at[2, g, pl.ds(0, 7)], g_recv.at[2, g])
        part, each = gathered[2, g], KINDS * 8
        for j in range(2):
            half = part[:, j * 8 : (j + 1) * 8]
            cuts = [half[i * KINDS : (i + 1) * KINDS].reshape(each, WIDE) for i in range(CUTS)]
            whole = jnp.concatenate(cuts, axis=1) if CUTS > 1 else cuts[0]
            out[j, :, g * each : (g + 1) * each] = whole.T

    plan = (
        (0.0, functools.partial(stage_x, 0)),
        (4.0, functools.partial(stage_relay, 0)),
        (5.0, stage_density),
        (7.3, stage_spread),
        (12.6, stage_collect),
        (15.4, lambda g: forward(g, 1, 7)),
        (15.5, lambda g: onward(g, 0)),
        (16.2, lambda g: forward(g, 2, 6)),
        (17.0, lambda g: forward(g, 3, 5)),
        (17.8, lambda g: forward(g, 4)),
        (18.2, lambda g: onward(g, 1, 7)),
        (18.3, stage_own),
        (19.0, lambda g: onward(g, 2, 6)),
        (19.8, lambda g: onward(g, 3, 5)),
        (20.6, lambda g: onward(g, 4)),
        (20.7, stage_next),
        (23.5, stage_far),
        (28.5, stage_join),
        (33.0, functools.partial(stage_x, 2)),
        (37.5, functools.partial(stage_relay, 2)),
        (40.8, stage_y),
        (45.6, stage_z),
        (51.0, stage_gather),
        (55.5, stage_out),
    )
    turns = [(at + g * APART, g, stage) for at, stage in plan for g in range(GROUPS)]
    for _, g, stage in sorted(turns, key=lambda turn: turn[0]):
        stage(g)
    for wait_send in sends:
        wait_send()


def step(fock, density, probe):
    f32, bf16 = jnp.float32, jnp.bfloat16
    vmem, dma = pltpu.VMEM, pltpu.SemaphoreType.DMA
    each = (PHASES, GROUPS)
    piece = (DEPTH, WIDE)
    return pl.pallas_call(
        kernel,
        out_shape=jax.ShapeDtypeStruct(probe.shape, f32),
        in_specs=[pl.BlockSpec(memory_space=pltpu.HBM)] * 3,
        out_specs=pl.BlockSpec(memory_space=pltpu.VMEM),
        scratch_shapes=[
            vmem(fock.shape, f32), vmem(density.shape, f32), vmem(probe.shape, f32),
            vmem((ROWS, 2 * COLS), bf16), vmem((ROWS, 2 * COLS), bf16),
            vmem((ROWS // COLS, 2 * COLS, COLS), bf16), vmem((ROWS // COLS, 2 * COLS, COLS), bf16),
            vmem((GROUPS, PIECES, *piece), f32),
            vmem((*each, 4, PIECES, *piece), f32),
            vmem((*each, 4, *piece), f32), vmem((*each, 4, *piece), f32),
            vmem((*each, PIECES, *piece), f32), vmem((*each, PIECES, *piece), f32),
            vmem((*each, PIECES, *piece), f32), vmem((*each, PIECES, *piece), f32),
            vmem((*each, 8, *piece), f32), vmem((GROUPS, 4, PIECES, *piece), f32),
            vmem((GROUPS, TALL, COLS), f32), vmem((*each, PIECES, *piece), f32),
            dma((6,)), dma((*each, 6)), dma((*each, 6)), dma((*each, PIECES)), dma((*each, PIECES)),
            dma((*each, 8)), dma(each), dma((*each, PIECES)), dma(each),
            dma((GROUPS, 8)), dma((GROUPS, 8)), dma((GROUPS, 3, 8)), dma((GROUPS, 3, 8)),
        ],
        compiler_params=pltpu.CompilerParams(
            collective_id=0, has_side_effects=True, vmem_limit_bytes=VMEM_LIMIT
        ),
    )(fock, density, probe)


def solution(mesh):
    return jax.shard_map(
        step,
        mesh=mesh,
        in_specs=(P(None, "row", "col"), P(None, "row", "col"), P(None, "col", None)),
        out_specs=P(None, "col", None),
        check_vma=False,
    )
```

time: 85.5 us -> 81.1 us (0.949)
  Pallas kernels: 83.7 us -> 79.3 us
    pallas_call x1, Pallas kernels: 83.7 us -> 79.3 us  [step(): pl.pallas_call(kernel, out_shape=jax.ShapeDtypeStruct(probe.shape, f32),...]
where the time goes in v4:
time: 81.1 us; the launch traced here: 80.9 us
  Pallas kernels  79.3 us (98%)
  local copies, waits for them, and re-layouts  1.67 us (2%)
    pallas_call x1, Pallas kernels, step(): pl.pallas_call(kernel, out_shape=jax.ShapeDtypeStruct(probe.shape, f32),...  79.3 us
    unnamed x1, local copies, waits for them, and re-layouts  1.67 us

profile of v4, /device:TPU:1, one launch (start us, length us, event | category | flops | bytes accessed | tf_op | source)
XLA Modules:
  0.0 80.9 jit_solution(11045295758568384044)
XLA Ops:
  0.0 79.3 %shard_map.37 = f32[2,256,128]{2,1,0:T(8,128)} custom-call(f32[2,1024,256]{2,1,0:T(8,128)} %fock_hbm.1, f32[2,1024,256]{2,1,0:T(8,128)} %density_hbm.1, f32[2,256,128]{2,1,0:T(8,128)} %probe_hbm.1), custom_call_target="tpu_custom_call" | custom-call | tf_op jit(solution)/shard_map/pallas_call | solution.py:350
  79.3 1.7 %copy.5 = f32[2,256,128]{2,1,0:T(8,128)} copy(f32[2,256,128]{2,1,0:T(8,128)} %shard_map.37) | data formatting | bytes 524288

commit v5 on v4

--- a/solution.py
+++ b/solution.py
@@ -20,7 +20,7 @@
 TALL = KINDS * DEPTH
 PHASES = 3
 VMEM_LIMIT = 60 * 1024 * 1024
-APART = 4.2
+APART = 5.6
 
 
 def split(value):
@@ -110,27 +110,22 @@
         for i in range(CUTS):
             start[:, i * KINDS : (i + 1) * KINDS, j * 8 : (j + 1) * 8, :] = probe_t[..., i * WIDE : (i + 1) * WIDE]
 
-    sends = []
-
     def send(source, target, send_sem, recv_sem, device):
         copy = pltpu.make_async_remote_copy(
             src_ref=source, dst_ref=target, send_sem=send_sem, recv_sem=recv_sem,
             device_id=device, device_id_type=MESH,
         )
         copy.start()
-        sends.append(copy.wait_send)
-
-    def landing(target, sem):
-        return pltpu.make_async_copy(target, target, sem).wait
 
     def landed(target, sem):
-        landing(target, sem)()
+        pltpu.make_async_copy(target, target, sem).wait()
 
     def store(box, value):
         for i in range(CUTS):
             box[i * KINDS : (i + 1) * KINDS] = value[:, i * WIDE : (i + 1) * WIDE].reshape(KINDS, DEPTH, WIDE)
 
-    A, B = pl.ds(0, 4), pl.ds(4, 4)
+    FIRST, LAST = pl.ds(0, 4), pl.ds(4, 4)
+    A, B = (pl.ds(0, 2), pl.ds(2, 2)), (pl.ds(4, 2), pl.ds(6, 2))
 
     def stage_x(phase, g):
         if phase == 0:
@@ -155,12 +150,13 @@
         one(0, 2)
         if phase == 0 and g == 0:
             pl.semaphore_wait(barrier, 16)
-        send(box.at[0, A], relay_a.at[phase, g], s.at[0], r.at[0], right)
-        send(box.at[0, B], relay_b.at[phase, g], s.at[1], r.at[1], left)
+        for i in range(2):
+            send(box.at[0, A[i]], relay_a.at[phase, g, i], s, r.at[i], right)
+            send(box.at[0, B[i]], relay_b.at[phase, g, i], s, r.at[2 + i], left)
         one(1, 1)
-        send(box.at[1, B], from_left.at[phase, g, B], s.at[2], r.at[2], right)
+        send(box.at[1, LAST], from_left.at[phase, g, LAST], s, r.at[4], right)
         one(2, 3)
-        send(box.at[2, A], from_right.at[phase, g, A], s.at[3], r.at[3], left)
+        send(box.at[2, FIRST], from_right.at[phase, g, FIRST], s, r.at[5], left)
         one(3, 0)
         if phase == 0:
             if g == 0:
@@ -173,19 +169,21 @@
     def stage_relay(phase, g):
         box = chunks.at[phase, g]
         s, r = x_send.at[phase, g], x_recv.at[phase, g]
-        landed(relay_a.at[phase, g], r.at[0])
-        box[1, 0:4] = box[1, 0:4] + relay_a[phase, g]
-        send(box.at[1, A], from_left.at[phase, g, A], s.at[4], r.at[4], right)
-        landed(relay_b.at[phase, g], r.at[1])
-        box[2, 4:8] = box[2, 4:8] + relay_b[phase, g]
-        send(box.at[2, B], from_right.at[phase, g, B], s.at[5], r.at[5], left)
+        for i in range(2):
+            landed(relay_a.at[phase, g, i], r.at[i])
+            box[1, A[i]] = box[1, A[i]] + relay_a[phase, g, i]
+            send(box.at[1, A[i]], from_left.at[phase, g, A[i]], s, r.at[6 + i], right)
+            landed(relay_b.at[phase, g, i], r.at[2 + i])
+            box[2, B[i]] = box[2, B[i]] + relay_b[phase, g, i]
+            send(box.at[2, B[i]], from_right.at[phase, g, B[i]], s, r.at[8 + i], left)
 
     def sum_x(phase, g):
         r = x_recv.at[phase, g]
-        landed(from_left.at[phase, g, B], r.at[2])
-        landed(from_right.at[phase, g, A], r.at[3])
-        landed(from_left.at[phase, g, A], r.at[4])
-        landed(from_right.at[phase, g, B], r.at[5])
+        landed(from_left.at[phase, g, LAST], r.at[4])
+        landed(from_right.at[phase, g, FIRST], r.at[5])
+        for i in range(2):
+            landed(from_left.at[phase, g, A[i]], r.at[6 + i])
+            landed(from_right.at[phase, g, B[i]], r.at[8 + i])
         summed[phase, g] = chunks[phase, g, 3] + from_left[phase, g] + from_right[phase, g]
 
     def sum_of(a):
@@ -195,16 +193,16 @@
         sum_x(0, g)
         for o in z_order:
             j = along_z(o)
-            send(summed.at[0, g, j], arrived.at[0, g, z], z_send.at[0, g, j], z_recv.at[0, g], (row, j * 4 + x))
+            send(summed.at[0, g, j], arrived.at[0, g, z], z_send.at[0, g], z_recv.at[0, g], (row, j * 4 + x))
         arrived[0, g, z] = summed[0, g, z]
 
     def stage_collect(g):
         landed(arrived.at[0, g, pl.ds(0, 7)], z_recv.at[0, g])
         mine = blocks.at[g, x, z]
         mine[...] = sum_of(arrived.at[0, g])
-        for o in z_order:
-            j = along_z(o)
-            send(mine, mine, zg_send.at[g, j], zg_recv.at[g, z], (row, j * 4 + x))
+        for o in z_order[::-1]:
+            j = along_z(o)
+            send(mine, mine, zg_send.at[g], zg_recv.at[g, z], (row, j * 4 + x))
         forward(g, 0)
 
     def forward(g, *offsets):
@@ -213,8 +211,8 @@
             piece = blocks.at[g, x, j]
             if o:
                 landed(piece, zg_recv.at[g, j])
-            send(piece, piece, xg_send.at[g, 0, j], xg_recv.at[g, 0, j], right)
-            send(piece, piece, xg_send.at[g, 1, j], xg_recv.at[g, 1, j], left)
+            send(piece, piece, xg_send.at[g], xg_recv.at[g, 0, j], right)
+            send(piece, piece, xg_send.at[g], xg_recv.at[g, 1, j], left)
 
     def onward(g, *offsets):
         for o in offsets:
@@ -222,7 +220,7 @@
             back, at, way = (3, 0, right) if o < 4 else (1, 1, left)
             piece = blocks.at[g, along_x(back), j]
             landed(piece, xg_recv.at[g, at, j])
-            send(piece, piece, xg_send.at[g, 2, j], xg_recv.at[g, 2, j], way)
+            send(piece, piece, xg_send.at[g], xg_recv.at[g, 2, j], way)
 
     def adjoint(g, ahead):
         block = along_x(ahead)
@@ -245,7 +243,7 @@
             landed(blocks.at[g, along_x(2), j], xg_recv.at[g, 2, j])
         store(summed.at[1, g], sums[g] + adjoint(g, 2))
         for p in peers:
-            send(summed.at[1, g, p], turned.at[1, g, row], y_send.at[1, g, p], y_recv.at[1, g, 0], (p, col))
+            send(summed.at[1, g, p], turned.at[1, g, row], y_send.at[1, g], y_recv.at[1, g, 0], (p, col))
         turned[1, g, row] = summed[1, g, row]
 
     def stage_join(g):
@@ -256,21 +254,21 @@
         mine = gathered.at[phase, g, row]
         mine[...] = value
         for p in peers:
-            send(mine, mine, g_send.at[phase, g, p], g_recv.at[phase, g], (p, col))
+            send(mine, mine, g_send.at[phase, g], g_recv.at[phase, g], (p, col))
 
     def to_z(g, block, source):
         @pl.when(block != z)
         def _():
             pltpu.make_async_remote_copy(
                 src_ref=source, dst_ref=arrived.at[2, g, z],
-                send_sem=z_send.at[2, g, block], recv_sem=z_recv.at[2, g],
+                send_sem=z_send.at[2, g], recv_sem=z_recv.at[2, g],
                 device_id=(row, block * 4 + x), device_id_type=MESH,
             ).start()
 
     def stage_y(g):
         sum_x(2, g)
         for p in peers:
-            send(summed.at[2, g, p], turned.at[2, g, row], y_send.at[2, g, p], y_recv.at[2, g, row], (p, col))
+            send(summed.at[2, g, p], turned.at[2, g, row], y_send.at[2, g], y_recv.at[2, g, row], (p, col))
         turned[2, g, row] = summed[2, g, row]
         to_z(g, row, summed.at[2, g, row])
 
@@ -280,8 +278,6 @@
             landed(piece, y_recv.at[2, g, p])
             to_z(g, p, piece)
         arrived[2, g, z] = turned[2, g, z]
-        for j in range(1, 8):
-            sends.append(landing(arrived.at[2, g, 0], z_send.at[2, g, along_z(j)]))
 
     def stage_gather(g):
         landed(arrived.at[2, g, pl.ds(0, 7)], z_recv.at[2, g])
@@ -309,37 +305,48 @@
             whole = jnp.concatenate(cuts, axis=1) if CUTS > 1 else cuts[0]
             out[j, :, g * each : (g + 1) * each] = whole.T
 
+    def sent(g):
+        seven = pl.ds(0, 7)
+        for phase in (0, 2):
+            landed(chunks.at[phase, g, pl.ds(0, 3)], x_send.at[phase, g])
+            landed(arrived.at[phase, g, seven], z_send.at[phase, g])
+        for phase in (1, 2):
+            landed(turned.at[phase, g, seven], y_send.at[phase, g])
+            landed(gathered.at[phase, g, seven], g_send.at[phase, g])
+        landed(arrived.at[0, g, seven], zg_send.at[g])
+        landed(blocks.at[g, pl.ds(0, 3)], xg_send.at[g])
+
     plan = (
-        (0.0, functools.partial(stage_x, 0)),
-        (4.0, functools.partial(stage_relay, 0)),
-        (5.0, stage_density),
-        (7.3, stage_spread),
-        (12.6, stage_collect),
-        (15.4, lambda g: forward(g, 1, 7)),
-        (15.5, lambda g: onward(g, 0)),
-        (16.2, lambda g: forward(g, 2, 6)),
-        (17.0, lambda g: forward(g, 3, 5)),
-        (17.8, lambda g: forward(g, 4)),
+        (0, functools.partial(stage_x, 0)),
+        (3.7, functools.partial(stage_relay, 0)),
+        (4.2, stage_density),
+        (7.0, stage_spread),
+        (12.1, stage_collect),
+        (15.5, lambda g: forward(g, 1, 7)),
+        (15.6, lambda g: onward(g, 0)),
+        (16.3, lambda g: forward(g, 2, 6)),
+        (17.1, lambda g: forward(g, 3, 5)),
+        (18.0, lambda g: forward(g, 4)),
+        (18.1, stage_own),
         (18.2, lambda g: onward(g, 1, 7)),
-        (18.3, stage_own),
         (19.0, lambda g: onward(g, 2, 6)),
-        (19.8, lambda g: onward(g, 3, 5)),
-        (20.6, lambda g: onward(g, 4)),
-        (20.7, stage_next),
-        (23.5, stage_far),
-        (28.5, stage_join),
-        (33.0, functools.partial(stage_x, 2)),
-        (37.5, functools.partial(stage_relay, 2)),
-        (40.8, stage_y),
-        (45.6, stage_z),
-        (51.0, stage_gather),
-        (55.5, stage_out),
+        (19.9, lambda g: onward(g, 3, 5)),
+        (20.9, lambda g: onward(g, 4)),
+        (21.1, stage_next),
+        (24, stage_far),
+        (29, stage_join),
+        (34, functools.partial(stage_x, 2)),
+        (38.3, functools.partial(stage_relay, 2)),
+        (42, stage_y),
+        (46.5, stage_z),
+        (51.5, stage_gather),
+        (56, stage_out),
     )
     turns = [(at + g * APART, g, stage) for at, stage in plan for g in range(GROUPS)]
     for _, g, stage in sorted(turns, key=lambda turn: turn[0]):
         stage(g)
-    for wait_send in sends:
-        wait_send()
+    for g in range(GROUPS):
+        sent(g)
 
 
 def step(fock, density, probe):
@@ -358,14 +365,14 @@
             vmem((ROWS // COLS, 2 * COLS, COLS), bf16), vmem((ROWS // COLS, 2 * COLS, COLS), bf16),
             vmem((GROUPS, PIECES, *piece), f32),
             vmem((*each, 4, PIECES, *piece), f32),
-            vmem((*each, 4, *piece), f32), vmem((*each, 4, *piece), f32),
+            vmem((*each, 2, 2, *piece), f32), vmem((*each, 2, 2, *piece), f32),
             vmem((*each, PIECES, *piece), f32), vmem((*each, PIECES, *piece), f32),
             vmem((*each, PIECES, *piece), f32), vmem((*each, PIECES, *piece), f32),
             vmem((*each, 8, *piece), f32), vmem((GROUPS, 4, PIECES, *piece), f32),
             vmem((GROUPS, TALL, COLS), f32), vmem((*each, PIECES, *piece), f32),
-            dma((6,)), dma((*each, 6)), dma((*each, 6)), dma((*each, PIECES)), dma((*each, PIECES)),
-            dma((*each, 8)), dma(each), dma((*each, PIECES)), dma(each),
-            dma((GROUPS, 8)), dma((GROUPS, 8)), dma((GROUPS, 3, 8)), dma((GROUPS, 3, 8)),
+            dma((6,)), dma(each), dma((*each, 10)), dma(each), dma((*each, PIECES)),
+            dma(each), dma(each), dma(each), dma(each),
+            dma((GROUPS,)), dma((GROUPS, 8)), dma((GROUPS,)), dma((GROUPS, 3, 8)),
         ],
         compiler_params=pltpu.CompilerParams(
             collective_id=0, has_side_effects=True, vmem_limit_bytes=VMEM_LIMIT

time: 81.1 us -> 76.8 us (0.947)
  Pallas kernels: 79.3 us -> 75 us
    pallas_call x1, Pallas kernels: 79.3 us -> 75 us  [step(): pl.pallas_call(kernel, out_shape=jax.ShapeDtypeStruct(probe.shape, f32),...]
where the time goes in v5:
time: 76.8 us; the launch traced here: 76.7 us
  Pallas kernels  75 us (98%)
  local copies, waits for them, and re-layouts  1.67 us (2%)
    pallas_call x1, Pallas kernels, step(): pl.pallas_call(kernel, out_shape=jax.ShapeDtypeStruct(probe.shape, f32),...  75 us
    unnamed x1, local copies, waits for them, and re-layouts  1.67 us

profile of v5, /device:TPU:1, one launch (start us, length us, event | category | flops | bytes accessed | tf_op | source)
XLA Modules:
  0.0 76.7 jit_solution(4536320176978878007)
XLA Ops:
  0.0 75.0 %shard_map.37 = f32[2,256,128]{2,1,0:T(8,128)} custom-call(f32[2,1024,256]{2,1,0:T(8,128)} %fock_hbm.1, f32[2,1024,256]{2,1,0:T(8,128)} %density_hbm.1, f32[2,256,128]{2,1,0:T(8,128)} %probe_hbm.1), custom_call_target="tpu_custom_call" | custom-call | tf_op jit(solution)/shard_map/pallas_call | solution.py:357
  75.0 1.7 %copy.5 = f32[2,256,128]{2,1,0:T(8,128)} copy(f32[2,256,128]{2,1,0:T(8,128)} %shard_map.37) | data formatting | bytes 524288

commit v6 on v5

--- a/solution.py
+++ b/solution.py
@@ -13,14 +13,24 @@
 COLS = 256
 PIECES = 8
 DEPTH = 16
-GROUPS = 2
+GROUPS = 4
 CUTS = GROUPS // 2
 WIDE = COLS // CUTS
 KINDS = PIECES // CUTS
 TALL = KINDS * DEPTH
 PHASES = 3
+WAVES = (0, 1, 2, 3, 4, 3, 2, 1)
+LATER, FAR = 5, 6
 VMEM_LIMIT = 60 * 1024 * 1024
-APART = 5.6
+ORDER = (
+    0, 4, 1, 8, 12, 2, 9, 13, 3, 16, 20, 10, 14, 21, 11, 15,
+    22, 24, 23, 25, 44, 28, 26, 32, 45, 36, 29, 48, 40, 64, 27, 33,
+    46, 52, 30, 37, 56, 34, 49, 60, 68, 41, 65, 38, 31, 47, 53, 42,
+    50, 66, 35, 57, 54, 72, 61, 69, 58, 39, 51, 43, 67, 62, 70, 55,
+    73, 59, 76, 63, 71, 74, 75, 77, 80, 78, 79, 84, 88, 81, 82, 92,
+    83, 85, 89, 86, 90, 87, 96, 91, 93, 94, 95, 97, 98, 100, 99, 104,
+    101, 102, 103, 105, 106, 107,
+)
 
 
 def split(value):
@@ -57,9 +67,9 @@
 
 def kernel(
     fock_hbm, density_hbm, probe_hbm, out,
-    fock, density, probe, fock_high, fock_low, density_high, density_low,
+    fock, density, probe, fock_high, fock_low, turned_high, turned_low, density_high, density_low,
     start, chunks, relay_a, relay_b, from_left, from_right, summed, turned, arrived, blocks, sums, gathered,
-    load_sem, x_send, x_recv, y_send, y_recv, z_send, z_recv, g_send, g_recv, zg_send, zg_recv, xg_send, xg_recv,
+    load_sem, x_send, x_recv, y_send, y_one, y_recv, z_send, z_recv, g_send, g_recv, zg_send, zg_recv, xg_send, xg_recv,
 ):
     row, col = lax.axis_index("row"), lax.axis_index("col")
     z, x = col // 4, lax.rem(col, 4)
@@ -131,11 +141,11 @@
         if phase == 0:
             vector = start[g]
         else:
-            landed(gathered.at[1, g, pl.ds(0, 7)], g_recv.at[1, g])
+            landed(gathered.at[1, g, pl.ds(0, 7)], g_recv.at[0, g])
             vector = gathered[1, g]
         high, low = factors(phase, vector)
         box = chunks.at[phase, g]
-        s, r = x_send.at[phase, g], x_recv.at[phase, g]
+        s, r = x_send.at[phase // 2], x_recv.at[phase // 2, g]
 
         def one(slot, ahead):
             rows = rows_of(along_x(ahead))
@@ -145,7 +155,11 @@
                     h, l = split(fock[j, rows, :])
                     fock_high[rows, j * COLS : (j + 1) * COLS] = h
                     fock_low[rows, j * COLS : (j + 1) * COLS] = l
-            store(box.at[slot], times(high, low, fock_high[rows, :], fock_low[rows, :], 1))
+                value = times(high, low, fock_high[rows, :], fock_low[rows, :], 1)
+            else:
+                block = along_x(ahead)
+                value = times(high, low, turned_high[block], turned_low[block], 0)
+            store(box.at[slot], value)
 
         one(0, 2)
         if phase == 0 and g == 0:
@@ -166,24 +180,20 @@
             def _():
                 box[3] = box[3] + start[g]
 
-    def stage_relay(phase, g):
+    def stage_relay(phase, i, g):
         box = chunks.at[phase, g]
-        s, r = x_send.at[phase, g], x_recv.at[phase, g]
-        for i in range(2):
-            landed(relay_a.at[phase, g, i], r.at[i])
-            box[1, A[i]] = box[1, A[i]] + relay_a[phase, g, i]
-            send(box.at[1, A[i]], from_left.at[phase, g, A[i]], s, r.at[6 + i], right)
-            landed(relay_b.at[phase, g, i], r.at[2 + i])
-            box[2, B[i]] = box[2, B[i]] + relay_b[phase, g, i]
-            send(box.at[2, B[i]], from_right.at[phase, g, B[i]], s, r.at[8 + i], left)
+        s, r = x_send.at[phase // 2], x_recv.at[phase // 2, g]
+        landed(relay_a.at[phase, g, i], r.at[i])
+        box[1, A[i]] = box[1, A[i]] + relay_a[phase, g, i]
+        send(box.at[1, A[i]], from_left.at[phase, g, A[i]], s, r.at[4], right)
+        landed(relay_b.at[phase, g, i], r.at[2 + i])
+        box[2, B[i]] = box[2, B[i]] + relay_b[phase, g, i]
+        send(box.at[2, B[i]], from_right.at[phase, g, B[i]], s, r.at[5], left)
 
     def sum_x(phase, g):
-        r = x_recv.at[phase, g]
-        landed(from_left.at[phase, g, LAST], r.at[4])
-        landed(from_right.at[phase, g, FIRST], r.at[5])
-        for i in range(2):
-            landed(from_left.at[phase, g, A[i]], r.at[6 + i])
-            landed(from_right.at[phase, g, B[i]], r.at[8 + i])
+        r = x_recv.at[phase // 2, g]
+        landed(from_left.at[phase, g], r.at[4])
+        landed(from_right.at[phase, g], r.at[5])
         summed[phase, g] = chunks[phase, g, 3] + from_left[phase, g] + from_right[phase, g]
 
     def sum_of(a):
@@ -193,7 +203,7 @@
         sum_x(0, g)
         for o in z_order:
             j = along_z(o)
-            send(summed.at[0, g, j], arrived.at[0, g, z], z_send.at[0, g], z_recv.at[0, g], (row, j * 4 + x))
+            send(summed.at[0, g, j], arrived.at[0, g, z], z_send.at[0], z_recv.at[0, g], (row, j * 4 + x))
         arrived[0, g, z] = summed[0, g, z]
 
     def stage_collect(g):
@@ -202,25 +212,25 @@
         mine[...] = sum_of(arrived.at[0, g])
         for o in z_order[::-1]:
             j = along_z(o)
-            send(mine, mine, zg_send.at[g], zg_recv.at[g, z], (row, j * 4 + x))
+            send(mine, mine, zg_send, zg_recv.at[g, min(o, 8 - o) - 1], (row, j * 4 + x))
         forward(g, 0)
 
     def forward(g, *offsets):
+        if offsets[0]:
+            landed(arrived.at[0, g, pl.ds(0, len(offsets))], zg_recv.at[g, offsets[0] - 1])
         for o in offsets:
             j = along_z(o)
             piece = blocks.at[g, x, j]
-            if o:
-                landed(piece, zg_recv.at[g, j])
-            send(piece, piece, xg_send.at[g], xg_recv.at[g, 0, j], right)
-            send(piece, piece, xg_send.at[g], xg_recv.at[g, 1, j], left)
+            first, second = (WAVES[o], LATER) if o < 4 else (LATER, WAVES[o])
+            send(piece, piece, xg_send, xg_recv.at[g, first], right)
+            send(piece, piece, xg_send, xg_recv.at[g, second], left)
 
     def onward(g, *offsets):
+        landed(arrived.at[0, g, pl.ds(0, len(offsets))], xg_recv.at[g, offsets[0]])
         for o in offsets:
-            j = along_z(o)
-            back, at, way = (3, 0, right) if o < 4 else (1, 1, left)
-            piece = blocks.at[g, along_x(back), j]
-            landed(piece, xg_recv.at[g, at, j])
-            send(piece, piece, xg_send.at[g], xg_recv.at[g, 2, j], way)
+            back, way = (3, right) if o < 4 else (1, left)
+            piece = blocks.at[g, along_x(back), along_z(o)]
+            send(piece, piece, xg_send, xg_recv.at[g, FAR], way)
 
     def adjoint(g, ahead):
         block = along_x(ahead)
@@ -231,57 +241,59 @@
         sums[g] = adjoint(g, 0)
 
     def stage_next(g):
-        for o in range(8):
-            j = along_z(o)
-            back, at = (1, 1) if o < 4 else (3, 0)
-            landed(blocks.at[g, along_x(back), j], xg_recv.at[g, at, j])
+        landed(blocks.at[g, 0], xg_recv.at[g, LATER])
         sums[g] = sums[g] + (adjoint(g, 1) + adjoint(g, 3))
 
     def stage_far(g):
-        for o in range(8):
-            j = along_z(o)
-            landed(blocks.at[g, along_x(2), j], xg_recv.at[g, 2, j])
+        landed(blocks.at[g, 0], xg_recv.at[g, FAR])
         store(summed.at[1, g], sums[g] + adjoint(g, 2))
         for p in peers:
-            send(summed.at[1, g, p], turned.at[1, g, row], y_send.at[1, g], y_recv.at[1, g, 0], (p, col))
+            send(summed.at[1, g, p], turned.at[1, g, row], y_send.at[0], y_one.at[g], (p, col))
         turned[1, g, row] = summed[1, g, row]
 
     def stage_join(g):
-        landed(turned.at[1, g, pl.ds(0, 7)], y_recv.at[1, g, 0])
+        landed(turned.at[1, g, pl.ds(0, 7)], y_one.at[g])
         gather(1, g, sum_of(turned.at[1, g]))
 
     def gather(phase, g, value):
         mine = gathered.at[phase, g, row]
         mine[...] = value
         for p in peers:
-            send(mine, mine, g_send.at[phase, g], g_recv.at[phase, g], (p, col))
+            send(mine, mine, g_send.at[phase - 1], g_recv.at[phase - 1, g], (p, col))
 
     def to_z(g, block, source):
         @pl.when(block != z)
         def _():
             pltpu.make_async_remote_copy(
                 src_ref=source, dst_ref=arrived.at[2, g, z],
-                send_sem=z_send.at[2, g], recv_sem=z_recv.at[2, g],
+                send_sem=z_send.at[1], recv_sem=z_recv.at[1, g],
                 device_id=(row, block * 4 + x), device_id_type=MESH,
             ).start()
 
     def stage_y(g):
         sum_x(2, g)
         for p in peers:
-            send(summed.at[2, g, p], turned.at[2, g, row], y_send.at[2, g], y_recv.at[2, g, row], (p, col))
+            send(summed.at[2, g, p], turned.at[2, g, row], y_send.at[1], y_recv.at[g, row], (p, col))
         turned[2, g, row] = summed[2, g, row]
         to_z(g, row, summed.at[2, g, row])
 
     def stage_z(g):
         for p in from_peers:
             piece = turned.at[2, g, p]
-            landed(piece, y_recv.at[2, g, p])
+            landed(piece, y_recv.at[g, p])
             to_z(g, p, piece)
         arrived[2, g, z] = turned[2, g, z]
 
     def stage_gather(g):
-        landed(arrived.at[2, g, pl.ds(0, 7)], z_recv.at[2, g])
+        landed(arrived.at[2, g, pl.ds(0, 7)], z_recv.at[1, g])
         gather(2, g, sum_of(arrived.at[2, g]) + gathered[1, g, row])
+
+    def stage_turn(g):
+        for i in range(ROWS // COLS):
+            for j in range(2):
+                h, l = split(fock[j, i * COLS : (i + 1) * COLS, :].T)
+                turned_high[i, j * COLS : (j + 1) * COLS] = h
+                turned_low[i, j * COLS : (j + 1) * COLS] = l
 
     def stage_density(g):
         if g == 0:
@@ -297,7 +309,7 @@
             lax.fori_loop(0, ROWS // COLS, part, 0)
 
     def stage_out(g):
-        landed(gathered.at[2, g, pl.ds(0, 7)], g_recv.at[2, g])
+        landed(gathered.at[2, g, pl.ds(0, 7)], g_recv.at[1, g])
         part, each = gathered[2, g], KINDS * 8
         for j in range(2):
             half = part[:, j * 8 : (j + 1) * 8]
@@ -305,48 +317,47 @@
             whole = jnp.concatenate(cuts, axis=1) if CUTS > 1 else cuts[0]
             out[j, :, g * each : (g + 1) * each] = whole.T
 
-    def sent(g):
-        seven = pl.ds(0, 7)
-        for phase in (0, 2):
-            landed(chunks.at[phase, g, pl.ds(0, 3)], x_send.at[phase, g])
-            landed(arrived.at[phase, g, seven], z_send.at[phase, g])
-        for phase in (1, 2):
-            landed(turned.at[phase, g, seven], y_send.at[phase, g])
-            landed(gathered.at[phase, g, seven], g_send.at[phase, g])
-        landed(arrived.at[0, g, seven], zg_send.at[g])
-        landed(blocks.at[g, pl.ds(0, 3)], xg_send.at[g])
+    def sent():
+        every, seven = pl.ds(0, GROUPS), pl.ds(0, 7)
+        for i in range(2):
+            landed(chunks.at[0, every, pl.ds(0, 3)], x_send.at[i])
+            for sem in (y_send, z_send, g_send):
+                landed(arrived.at[0, every, seven], sem.at[i])
+        landed(arrived.at[0, every, seven], zg_send)
+        landed(blocks.at[every, pl.ds(0, 3)], xg_send)
 
     plan = (
-        (0, functools.partial(stage_x, 0)),
-        (3.7, functools.partial(stage_relay, 0)),
-        (4.2, stage_density),
-        (7.0, stage_spread),
-        (12.1, stage_collect),
-        (15.5, lambda g: forward(g, 1, 7)),
-        (15.6, lambda g: onward(g, 0)),
-        (16.3, lambda g: forward(g, 2, 6)),
-        (17.1, lambda g: forward(g, 3, 5)),
-        (18.0, lambda g: forward(g, 4)),
-        (18.1, stage_own),
-        (18.2, lambda g: onward(g, 1, 7)),
-        (19.0, lambda g: onward(g, 2, 6)),
-        (19.9, lambda g: onward(g, 3, 5)),
-        (20.9, lambda g: onward(g, 4)),
-        (21.1, stage_next),
-        (24, stage_far),
-        (29, stage_join),
-        (34, functools.partial(stage_x, 2)),
-        (38.3, functools.partial(stage_relay, 2)),
-        (42, stage_y),
-        (46.5, stage_z),
-        (51.5, stage_gather),
-        (56, stage_out),
+        functools.partial(stage_x, 0),
+        stage_turn,
+        functools.partial(stage_relay, 0, 0),
+        functools.partial(stage_relay, 0, 1),
+        stage_density,
+        stage_spread,
+        stage_collect,
+        lambda g: forward(g, 1, 7),
+        lambda g: forward(g, 2, 6),
+        lambda g: forward(g, 3, 5),
+        lambda g: forward(g, 4),
+        lambda g: onward(g, 0),
+        lambda g: onward(g, 1, 7),
+        lambda g: onward(g, 2, 6),
+        lambda g: onward(g, 3, 5),
+        lambda g: onward(g, 4),
+        stage_own,
+        stage_next,
+        stage_far,
+        stage_join,
+        functools.partial(stage_x, 2),
+        functools.partial(stage_relay, 2, 0),
+        functools.partial(stage_relay, 2, 1),
+        stage_y,
+        stage_z,
+        stage_gather,
+        stage_out,
     )
-    turns = [(at + g * APART, g, stage) for at, stage in plan for g in range(GROUPS)]
-    for _, g, stage in sorted(turns, key=lambda turn: turn[0]):
-        stage(g)
-    for g in range(GROUPS):
-        sent(g)
+    for turn in ORDER:
+        plan[turn // 4](turn % 4)
+    sent()
 
 
 def step(fock, density, probe):
@@ -363,6 +374,7 @@
             vmem(fock.shape, f32), vmem(density.shape, f32), vmem(probe.shape, f32),
             vmem((ROWS, 2 * COLS), bf16), vmem((ROWS, 2 * COLS), bf16),
             vmem((ROWS // COLS, 2 * COLS, COLS), bf16), vmem((ROWS // COLS, 2 * COLS, COLS), bf16),
+            vmem((ROWS // COLS, 2 * COLS, COLS), bf16), vmem((ROWS // COLS, 2 * COLS, COLS), bf16),
             vmem((GROUPS, PIECES, *piece), f32),
             vmem((*each, 4, PIECES, *piece), f32),
             vmem((*each, 2, 2, *piece), f32), vmem((*each, 2, 2, *piece), f32),
@@ -370,9 +382,9 @@
             vmem((*each, PIECES, *piece), f32), vmem((*each, PIECES, *piece), f32),
             vmem((*each, 8, *piece), f32), vmem((GROUPS, 4, PIECES, *piece), f32),
             vmem((GROUPS, TALL, COLS), f32), vmem((*each, PIECES, *piece), f32),
-            dma((6,)), dma(each), dma((*each, 10)), dma(each), dma((*each, PIECES)),
-            dma(each), dma(each), dma(each), dma(each),
-            dma((GROUPS,)), dma((GROUPS, 8)), dma((GROUPS,)), dma((GROUPS, 3, 8)),
+            dma((6,)), dma((2,)), dma((2, GROUPS, 6)), dma((2,)), dma((GROUPS,)), dma((GROUPS, PIECES)),
+            dma((2,)), dma((2, GROUPS)), dma((2,)), dma((2, GROUPS)),
+            dma, dma((GROUPS, 4)), dma, dma((GROUPS, 7)),
         ],
         compiler_params=pltpu.CompilerParams(
             collective_id=0, has_side_effects=True, vmem_limit_bytes=VMEM_LIMIT

time: 76.8 us -> 75 us (0.977)
  Pallas kernels: 75 us -> 73.2 us
    pallas_call x1, Pallas kernels: 75 us -> 73.2 us  [step(): pl.pallas_call(kernel, out_shape=jax.ShapeDtypeStruct(probe.shape, f32),...]
where the time goes in v6:
time: 75 us; the launch traced here: 74.8 us
  Pallas kernels  73.2 us (98%)
  local copies, waits for them, and re-layouts  1.67 us (2%)
    pallas_call x1, Pallas kernels, step(): pl.pallas_call(kernel, out_shape=jax.ShapeDtypeStruct(probe.shape, f32),...  73.2 us
    unnamed x1, local copies, waits for them, and re-layouts  1.67 us

profile of v6, /device:TPU:1, one launch (start us, length us, event | category | flops | bytes accessed | tf_op | source)
XLA Modules:
  0.0 74.8 jit_solution(9922389008501679352)
XLA Ops:
  0.0 73.2 %shard_map.37 = f32[2,256,128]{2,1,0:T(8,128)} custom-call(f32[2,1024,256]{2,1,0:T(8,128)} %fock_hbm.1, f32[2,1024,256]{2,1,0:T(8,128)} %density_hbm.1, f32[2,256,128]{2,1,0:T(8,128)} %probe_hbm.1), custom_call_target="tpu_custom_call" | custom-call | tf_op jit(solution)/shard_map/pallas_call | solution.py:368
  73.2 1.7 %copy.5 = f32[2,256,128]{2,1,0:T(8,128)} copy(f32[2,256,128]{2,1,0:T(8,128)} %shard_map.37) | data formatting | bytes 524288

commit v7 on v6

--- a/solution.py
+++ b/solution.py
@@ -19,17 +19,13 @@
 KINDS = PIECES // CUTS
 TALL = KINDS * DEPTH
 PHASES = 3
-WAVES = (0, 1, 2, 3, 4, 3, 2, 1)
-LATER, FAR = 5, 6
 VMEM_LIMIT = 60 * 1024 * 1024
 ORDER = (
-    0, 4, 1, 8, 12, 2, 9, 13, 3, 16, 20, 10, 14, 21, 11, 15,
-    22, 24, 23, 25, 44, 28, 26, 32, 45, 36, 29, 48, 40, 64, 27, 33,
-    46, 52, 30, 37, 56, 34, 49, 60, 68, 41, 65, 38, 31, 47, 53, 42,
-    50, 66, 35, 57, 54, 72, 61, 69, 58, 39, 51, 43, 67, 62, 70, 55,
-    73, 59, 76, 63, 71, 74, 75, 77, 80, 78, 79, 84, 88, 81, 82, 92,
-    83, 85, 89, 86, 90, 87, 96, 91, 93, 94, 95, 97, 98, 100, 99, 104,
-    101, 102, 103, 105, 106, 107,
+    0, 4, 1, 2, 3, 8, 12, 13, 16, 14, 17, 20, 15, 24, 28, 21,
+    32, 36, 18, 25, 29, 33, 37, 19, 22, 40, 44, 26, 30, 41, 23, 45,
+    34, 38, 27, 48, 31, 35, 39, 42, 49, 46, 52, 43, 47, 53, 50, 51,
+    56, 54, 57, 55, 60, 61, 58, 59, 64, 62, 65, 63, 68, 69, 66, 67,
+    70, 71,
 )
 
 
@@ -68,7 +64,7 @@
 def kernel(
     fock_hbm, density_hbm, probe_hbm, out,
     fock, density, probe, fock_high, fock_low, turned_high, turned_low, density_high, density_low,
-    start, chunks, relay_a, relay_b, from_left, from_right, summed, turned, arrived, blocks, sums, gathered,
+    start, chunks, from_far, from_left, from_right, summed, turned, arrived, blocks, sums, gathered,
     load_sem, x_send, x_recv, y_send, y_one, y_recv, z_send, z_recv, g_send, g_recv, zg_send, zg_recv, xg_send, xg_recv,
 ):
     row, col = lax.axis_index("row"), lax.axis_index("col")
@@ -76,6 +72,7 @@
     y, core = row // 2, lax.rem(row, 2)
     right = (row, z * 4 + lax.rem(x + 1, 4))
     left = (row, z * 4 + lax.rem(x + 3, 4))
+    far = (row, z * 4 + lax.rem(x + 2, 4))
 
     def along_x(ahead):
         return lax.rem(x + ahead, 4)
@@ -99,6 +96,7 @@
         hello(row, along_z(j) * 4 + x)
     for p in peers:
         hello(p, col)
+    hello(*far)
     hello(*right)
     hello(*left)
 
@@ -133,9 +131,6 @@
     def store(box, value):
         for i in range(CUTS):
             box[i * KINDS : (i + 1) * KINDS] = value[:, i * WIDE : (i + 1) * WIDE].reshape(KINDS, DEPTH, WIDE)
-
-    FIRST, LAST = pl.ds(0, 4), pl.ds(4, 4)
-    A, B = (pl.ds(0, 2), pl.ds(2, 2)), (pl.ds(4, 2), pl.ds(6, 2))
 
     def stage_x(phase, g):
         if phase == 0:
@@ -163,14 +158,12 @@
 
         one(0, 2)
         if phase == 0 and g == 0:
-            pl.semaphore_wait(barrier, 16)
-        for i in range(2):
-            send(box.at[0, A[i]], relay_a.at[phase, g, i], s, r.at[i], right)
-            send(box.at[0, B[i]], relay_b.at[phase, g, i], s, r.at[2 + i], left)
+            pl.semaphore_wait(barrier, 17)
+        send(box.at[0], from_far.at[phase, g], s, r, far)
         one(1, 1)
-        send(box.at[1, LAST], from_left.at[phase, g, LAST], s, r.at[4], right)
+        send(box.at[1], from_left.at[phase, g], s, r, right)
         one(2, 3)
-        send(box.at[2, FIRST], from_right.at[phase, g, FIRST], s, r.at[5], left)
+        send(box.at[2], from_right.at[phase, g], s, r, left)
         one(3, 0)
         if phase == 0:
             if g == 0:
@@ -180,21 +173,10 @@
             def _():
                 box[3] = box[3] + start[g]
 
-    def stage_relay(phase, i, g):
-        box = chunks.at[phase, g]
-        s, r = x_send.at[phase // 2], x_recv.at[phase // 2, g]
-        landed(relay_a.at[phase, g, i], r.at[i])
-        box[1, A[i]] = box[1, A[i]] + relay_a[phase, g, i]
-        send(box.at[1, A[i]], from_left.at[phase, g, A[i]], s, r.at[4], right)
-        landed(relay_b.at[phase, g, i], r.at[2 + i])
-        box[2, B[i]] = box[2, B[i]] + relay_b[phase, g, i]
-        send(box.at[2, B[i]], from_right.at[phase, g, B[i]], s, r.at[5], left)
-
     def sum_x(phase, g):
-        r = x_recv.at[phase // 2, g]
-        landed(from_left.at[phase, g], r.at[4])
-        landed(from_right.at[phase, g], r.at[5])
-        summed[phase, g] = chunks[phase, g, 3] + from_left[phase, g] + from_right[phase, g]
+        landed(chunks.at[phase, g, pl.ds(0, 3)], x_recv.at[phase // 2, g])
+        near = from_left[phase, g] + from_right[phase, g]
+        summed[phase, g] = (chunks[phase, g, 3] + from_far[phase, g]) + near
 
     def sum_of(a):
         return ((a[0] + a[1]) + (a[2] + a[3])) + ((a[4] + a[5]) + (a[6] + a[7]))
@@ -221,16 +203,9 @@
         for o in offsets:
             j = along_z(o)
             piece = blocks.at[g, x, j]
-            first, second = (WAVES[o], LATER) if o < 4 else (LATER, WAVES[o])
-            send(piece, piece, xg_send, xg_recv.at[g, first], right)
-            send(piece, piece, xg_send, xg_recv.at[g, second], left)
-
-    def onward(g, *offsets):
-        landed(arrived.at[0, g, pl.ds(0, len(offsets))], xg_recv.at[g, offsets[0]])
-        for o in offsets:
-            back, way = (3, right) if o < 4 else (1, left)
-            piece = blocks.at[g, along_x(back), along_z(o)]
-            send(piece, piece, xg_send, xg_recv.at[g, FAR], way)
+            send(piece, piece, xg_send, xg_recv.at[g, 1], far)
+            send(piece, piece, xg_send, xg_recv.at[g, 0], right)
+            send(piece, piece, xg_send, xg_recv.at[g, 0], left)
 
     def adjoint(g, ahead):
         block = along_x(ahead)
@@ -241,11 +216,11 @@
         sums[g] = adjoint(g, 0)
 
     def stage_next(g):
-        landed(blocks.at[g, 0], xg_recv.at[g, LATER])
+        landed(blocks.at[g, pl.ds(0, 2)], xg_recv.at[g, 0])
         sums[g] = sums[g] + (adjoint(g, 1) + adjoint(g, 3))
 
     def stage_far(g):
-        landed(blocks.at[g, 0], xg_recv.at[g, FAR])
+        landed(blocks.at[g, 0], xg_recv.at[g, 1])
         store(summed.at[1, g], sums[g] + adjoint(g, 2))
         for p in peers:
             send(summed.at[1, g, p], turned.at[1, g, row], y_send.at[0], y_one.at[g], (p, col))
@@ -329,8 +304,6 @@
     plan = (
         functools.partial(stage_x, 0),
         stage_turn,
-        functools.partial(stage_relay, 0, 0),
-        functools.partial(stage_relay, 0, 1),
         stage_density,
         stage_spread,
         stage_collect,
@@ -338,18 +311,11 @@
         lambda g: forward(g, 2, 6),
         lambda g: forward(g, 3, 5),
         lambda g: forward(g, 4),
-        lambda g: onward(g, 0),
-        lambda g: onward(g, 1, 7),
-        lambda g: onward(g, 2, 6),
-        lambda g: onward(g, 3, 5),
-        lambda g: onward(g, 4),
         stage_own,
         stage_next,
         stage_far,
         stage_join,
         functools.partial(stage_x, 2),
-        functools.partial(stage_relay, 2, 0),
-        functools.partial(stage_relay, 2, 1),
         stage_y,
         stage_z,
         stage_gather,
@@ -377,14 +343,14 @@
             vmem((ROWS // COLS, 2 * COLS, COLS), bf16), vmem((ROWS // COLS, 2 * COLS, COLS), bf16),
             vmem((GROUPS, PIECES, *piece), f32),
             vmem((*each, 4, PIECES, *piece), f32),
-            vmem((*each, 2, 2, *piece), f32), vmem((*each, 2, 2, *piece), f32),
+            vmem((*each, PIECES, *piece), f32),
             vmem((*each, PIECES, *piece), f32), vmem((*each, PIECES, *piece), f32),
             vmem((*each, PIECES, *piece), f32), vmem((*each, PIECES, *piece), f32),
             vmem((*each, 8, *piece), f32), vmem((GROUPS, 4, PIECES, *piece), f32),
             vmem((GROUPS, TALL, COLS), f32), vmem((*each, PIECES, *piece), f32),
-            dma((6,)), dma((2,)), dma((2, GROUPS, 6)), dma((2,)), dma((GROUPS,)), dma((GROUPS, PIECES)),
+            dma((6,)), dma((2,)), dma((2, GROUPS)), dma((2,)), dma((GROUPS,)), dma((GROUPS, PIECES)),
             dma((2,)), dma((2, GROUPS)), dma((2,)), dma((2, GROUPS)),
-            dma, dma((GROUPS, 4)), dma, dma((GROUPS, 7)),
+            dma, dma((GROUPS, 4)), dma, dma((GROUPS, 2)),
         ],
         compiler_params=pltpu.CompilerParams(
             collective_id=0, has_side_effects=True, vmem_limit_bytes=VMEM_LIMIT

time: 75 us -> 69.8 us (0.931)
  Pallas kernels: 73.2 us -> 68 us
    pallas_call x1, Pallas kernels: 73.2 us -> 68 us  [step(): pl.pallas_call(kernel, out_shape=jax.ShapeDtypeStruct(probe.shape, f32),...]
where the time goes in v7:
time: 69.8 us; the launch traced here: 69.6 us
  Pallas kernels  68 us (97%)
  local copies, waits for them, and re-layouts  1.67 us (2%)
    pallas_call x1, Pallas kernels, step(): pl.pallas_call(kernel, out_shape=jax.ShapeDtypeStruct(probe.shape, f32),...  68 us
    unnamed x1, local copies, waits for them, and re-layouts  1.67 us

profile of v7, /device:TPU:1, one launch (start us, length us, event | category | flops | bytes accessed | tf_op | source)
XLA Modules:
  0.0 69.6 jit_solution(12304111110917450319)
XLA Ops:
  0.0 68.0 %shard_map.37 = f32[2,256,128]{2,1,0:T(8,128)} custom-call(f32[2,1024,256]{2,1,0:T(8,128)} %fock_hbm.1, f32[2,1024,256]{2,1,0:T(8,128)} %density_hbm.1, f32[2,256,128]{2,1,0:T(8,128)} %probe_hbm.1), custom_call_target="tpu_custom_call" | custom-call | tf_op jit(solution)/shard_map/pallas_call | solution.py:334
  68.0 1.7 %copy.5 = f32[2,256,128]{2,1,0:T(8,128)} copy(f32[2,256,128]{2,1,0:T(8,128)} %shard_map.37) | data formatting | bytes 524288

commit v8 on v7

--- a/solution.py
+++ b/solution.py
@@ -21,11 +21,11 @@
 PHASES = 3
 VMEM_LIMIT = 60 * 1024 * 1024
 ORDER = (
-    0, 4, 1, 2, 3, 8, 12, 13, 16, 14, 17, 20, 15, 24, 28, 21,
-    32, 36, 18, 25, 29, 33, 37, 19, 22, 40, 44, 26, 30, 41, 23, 45,
-    34, 38, 27, 48, 31, 35, 39, 42, 49, 46, 52, 43, 47, 53, 50, 51,
-    56, 54, 57, 55, 60, 61, 58, 59, 64, 62, 65, 63, 68, 69, 66, 67,
-    70, 71,
+    0, 4, 1, 8, 12, 2, 3, 13, 16, 14, 17, 15, 20, 24, 28, 32,
+    21, 36, 18, 25, 29, 33, 19, 40, 22, 44, 26, 37, 30, 34, 23, 41,
+    45, 27, 48, 38, 31, 35, 39, 42, 46, 49, 52, 43, 47, 50, 53, 51,
+    54, 55, 56, 57, 58, 60, 61, 59, 62, 63, 64, 66, 68, 65, 67, 70,
+    69, 71,
 )
 
 

time: 69.8 us -> 68 us (0.974)
  Pallas kernels: 68 us -> 66.2 us
    pallas_call x1, Pallas kernels: 68 us -> 66.2 us  [step(): pl.pallas_call(kernel, out_shape=jax.ShapeDtypeStruct(probe.shape, f32),...]
where the time goes in v8:
time: 68 us; the launch traced here: 67.9 us
  Pallas kernels  66.2 us (97%)
  local copies, waits for them, and re-layouts  1.67 us (2%)
    pallas_call x1, Pallas kernels, step(): pl.pallas_call(kernel, out_shape=jax.ShapeDtypeStruct(probe.shape, f32),...  66.2 us
    unnamed x1, local copies, waits for them, and re-layouts  1.67 us

profile of v8, /device:TPU:1, one launch (start us, length us, event | category | flops | bytes accessed | tf_op | source)
XLA Modules:
  0.0 67.9 jit_solution(2826554356472209534)
XLA Ops:
  0.0 66.2 %shard_map.37 = f32[2,256,128]{2,1,0:T(8,128)} custom-call(f32[2,1024,256]{2,1,0:T(8,128)} %fock_hbm.1, f32[2,1024,256]{2,1,0:T(8,128)} %density_hbm.1, f32[2,256,128]{2,1,0:T(8,128)} %probe_hbm.1), custom_call_target="tpu_custom_call" | custom-call | tf_op jit(solution)/shard_map/pallas_call | solution.py:334
  66.2 1.7 %copy.5 = f32[2,256,128]{2,1,0:T(8,128)} copy(f32[2,256,128]{2,1,0:T(8,128)} %shard_map.37) | data formatting | bytes 524288

commit v9 on v8

--- a/solution.py
+++ b/solution.py
@@ -19,7 +19,7 @@
 KINDS = PIECES // CUTS
 TALL = KINDS * DEPTH
 PHASES = 3
-VMEM_LIMIT = 60 * 1024 * 1024
+VMEM_LIMIT = 54784 * 1024
 ORDER = (
     0, 4, 1, 8, 12, 2, 3, 13, 16, 14, 17, 15, 20, 24, 28, 32,
     21, 36, 18, 25, 29, 33, 19, 40, 22, 44, 26, 37, 30, 34, 23, 41,
@@ -84,7 +84,8 @@
         return lax.rem(y + dy, 4) * 2 + lax.rem(core + dc, 2)
 
     peers = [peer(*d) for d in ((2, 0), (2, 1), (1, 0), (3, 0), (1, 1), (3, 1), (0, 1))]
-    from_peers = [peer(*d) for d in ((0, 1), (1, 0), (3, 0), (1, 1), (3, 1), (2, 0), (2, 1))]
+    waves = [[peer(*d) for d in wave] for wave in (((0, 1),), ((1, 0), (3, 0), (1, 1), (3, 1)), ((2, 0), (2, 1)))]
+    wave_of = (2, 2, 1, 1, 1, 1, 0)
     z_order = (4, 3, 5, 2, 6, 1, 7)
 
     barrier = pltpu.get_barrier_semaphore()
@@ -247,16 +248,16 @@
 
     def stage_y(g):
         sum_x(2, g)
-        for p in peers:
-            send(summed.at[2, g, p], turned.at[2, g, row], y_send.at[1], y_recv.at[g, row], (p, col))
+        for p, wave in zip(peers, wave_of):
+            send(summed.at[2, g, p], turned.at[2, g, row], y_send.at[1], y_recv.at[g, wave], (p, col))
         turned[2, g, row] = summed[2, g, row]
         to_z(g, row, summed.at[2, g, row])
 
     def stage_z(g):
-        for p in from_peers:
-            piece = turned.at[2, g, p]
-            landed(piece, y_recv.at[g, p])
-            to_z(g, p, piece)
+        for i, wave in enumerate(waves):
+            landed(arrived.at[2, g, pl.ds(0, len(wave))], y_recv.at[g, i])
+            for p in wave:
+                to_z(g, p, turned.at[2, g, p])
         arrived[2, g, z] = turned[2, g, z]
 
     def stage_gather(g):
@@ -348,7 +349,7 @@
             vmem((*each, PIECES, *piece), f32), vmem((*each, PIECES, *piece), f32),
             vmem((*each, 8, *piece), f32), vmem((GROUPS, 4, PIECES, *piece), f32),
             vmem((GROUPS, TALL, COLS), f32), vmem((*each, PIECES, *piece), f32),
-            dma((6,)), dma((2,)), dma((2, GROUPS)), dma((2,)), dma((GROUPS,)), dma((GROUPS, PIECES)),
+            dma((6,)), dma((2,)), dma((2, GROUPS)), dma((2,)), dma((GROUPS,)), dma((GROUPS, 3)),
             dma((2,)), dma((2, GROUPS)), dma((2,)), dma((2, GROUPS)),
             dma, dma((GROUPS, 4)), dma, dma((GROUPS, 2)),
         ],

time: 68 us -> 66.1 us (0.972)
  local copies, waits for them, and re-layouts: 1.67 us -> 0.71 us
  Pallas kernels: 66.2 us -> 65.3 us
    unnamed x1, local copies, waits for them, and re-layouts: 1.67 us -> 0.71 us
    pallas_call x1, Pallas kernels: 66.2 us -> 65.3 us  [step(): pl.pallas_call(kernel, out_shape=jax.ShapeDtypeStruct(probe.shape, f32),...]
where the time goes in v9:
time: 66.1 us; the launch traced here: 66 us
  Pallas kernels  65.3 us (99%)
  local copies, waits for them, and re-layouts  0.71 us (1%)
    pallas_call x1, Pallas kernels, step(): pl.pallas_call(kernel, out_shape=jax.ShapeDtypeStruct(probe.shape, f32),...  65.3 us

profile of v9, /device:TPU:1, one launch (start us, length us, event | category | flops | bytes accessed | tf_op | source)
XLA Modules:
  0.0 66.0 jit_solution(13886652043846600958)
XLA Ops:
  0.0 65.3 %shard_map.37 = f32[2,256,128]{2,1,0:T(8,128)S(1)} custom-call(f32[2,1024,256]{2,1,0:T(8,128)} %fock_hbm.1, f32[2,1024,256]{2,1,0:T(8,128)} %density_hbm.1, f32[2,256,128]{2,1,0:T(8,128)} %probe_hbm.1), custom_call_target="tpu_custom_call" | custom-call | tf_op jit(solution)/shard_map/pallas_call | solution.py:335
  65.3 0.7 %copy.5 = f32[2,256,128]{2,1,0:T(8,128)} copy(f32[2,256,128]{2,1,0:T(8,128)S(1)} %shard_map.37) | data formatting | bytes 524288
